TPU v7x, 512 devices: a whole 4x8x8 slice. The times are simulated.
512 devices in a mesh: row: 16 (over y, core), col: 32 (over z, x).
Axes of the slice: x: 4, y: 8, z: 8, core: 2. Of those that a mesh axis runs over, the one named last changes fastest.
Arguments:
- singles: bfloat16 [1536, 384], P(('row', 'col')), may hold values from -6 to 6
- pair: float32 [1536, 1536, 128], P('row', 'col'), may hold values from -48 to 48
- frames: float32 [1536, 12], P(('row', 'col')), may hold values from -9 to 9, as said below
- w_query: bfloat16 [384, 336], replicated, may hold values from -0.3125 to 0.3125
- w_keyval: bfloat16 [384, 816], replicated, may hold values from -0.3125 to 0.3125
- w_bias: float32 [128, 12], replicated, may hold values from -1 to 1
- head_weights: float32 [12], replicated, may hold values from -2 to 1
- w_out: bfloat16 [2112, 384], replicated, may hold values from -0.125 to 0.125
Outputs:
- update: float32 [1536, 384], P(('row', 'col'))
Inputs may be any that keep to these rules, and one draw needn't show every extreme that they name: `frames`: the first nine entries of a row are a rotation matrix in row-major order, the last three a translation.
All inputs are finite; a program needn't handle non-finite values.
Results may differ from a plain program's by a relative error of at most 0.0029.
Values sent between devices are 32-bit elements; how exact they have to be, the bound alone decides.
A program may use at most 64 MiB of HBM per device.

v0:
```python
import functools
import math

import jax
import jax.numpy as jnp
from jax import lax
from jax.experimental import pallas as pl
from jax.experimental.pallas import tpu as pltpu
from jax.sharding import PartitionSpec as P

CS = 384
CZ = 128
H = 12
CH = 16
PQ = 4
PV = 8

HP = 16
LANES = 128
HIGHEST = lax.Precision.HIGHEST
MESH = pl.DeviceIdType.MESH
NT = (((1,), (1,)), ((), ()))
NN = (((1,), (0,)), ((), ()))


def round_up(value, step):
    return (value + step - 1) // step * step


def dot_exact(left, right, dims):
    return lax.dot_general(
        left, right, dims, precision=HIGHEST, preferred_element_type=jnp.float32
    )


def head_mask(width, offset, per_head, heads_period):
    feature = lax.broadcasted_iota(jnp.int32, (HP, width), 1) - offset
    head = lax.broadcasted_iota(jnp.int32, (HP, width), 0)
    return (feature % heads_period) // per_head == head


def moved_points(frame, local, width):
    parts = [local[:, b * width : (b + 1) * width] for b in range(3)]
    return [
        frame[:, 3 * a : 3 * a + 1] * parts[0]
        + frame[:, 3 * a + 1 : 3 * a + 2] * parts[1]
        + frame[:, 3 * a + 2 : 3 * a + 3] * parts[2]
        + frame[:, 9 + a : 10 + a]
        for a in range(3)
    ]


def moved_columns(frame, local, width):
    parts = [local[b * width : (b + 1) * width] for b in range(3)]
    return [
        frame[3 * a : 3 * a + 1] * parts[0]
        + frame[3 * a + 1 : 3 * a + 2] * parts[1]
        + frame[3 * a + 2 : 3 * a + 3] * parts[2]
        + frame[9 + a : 10 + a]
        for a in range(3)
    ]


def kernel(
    sizes,
    singles_ref,
    frames_ref,
    w_bias_ref,
    heads_ref,
    pair_hbm,
    w_query_hbm,
    w_keyval_hbm,
    w_out_hbm,
    out_ref,
    x_all,
    pair_raw,
    pair_own,
    pair_all,
    w_query_ref,
    w_keyval_ref,
    w_out_ref,
    k_feat,
    v_feat,
    load_sem,
    x_send,
    x_recv,
    p_send,
    p_recv,
):
    row_devs, col_devs = sizes
    devices = row_devs * col_devs
    rows = singles_ref.shape[0]
    keys = pair_own.shape[1]
    key_pad = round_up(keys, 8)
    slots = col_devs * key_pad
    row = lax.axis_index("row")
    col = lax.axis_index("col")
    me = row * col_devs + col

    loads = [
        pltpu.make_async_copy(pair_hbm, pair_raw, load_sem.at[0]),
        pltpu.make_async_copy(w_query_hbm, w_query_ref, load_sem.at[1]),
        pltpu.make_async_copy(w_keyval_hbm, w_keyval_ref, load_sem.at[2]),
        pltpu.make_async_copy(w_out_hbm, w_out_ref, load_sem.at[3]),
    ]
    for load in loads:
        load.start()

    barrier = pltpu.get_barrier_semaphore()
    core = lax.rem(row, 2)
    place_in_plane = row // 2 * col_devs + col
    plane = devices // 2

    def in_plane(step):
        index = lax.rem(place_in_plane + step, plane)
        return (index // col_devs * 2 + core, lax.rem(index, col_devs))

    def partner_of(peer):
        return (peer[0] // 2 * 2 + 1 - lax.rem(peer[0], 2), peer[1])

    def number_of(peer):
        return peer[0] * col_devs + peer[1]

    here = (row, col)

    def greet_one(peer):
        pl.semaphore_signal(barrier, inc=1, device_id=peer, device_id_type=MESH)

    def greet(step, carry):
        greet_one(in_plane(step))
        return carry

    lax.fori_loop(1, plane, greet, 0)
    greet_one(partner_of(here))

    def slot_of(device):
        first = device * rows
        return first // keys * key_pad + lax.rem(first, keys)

    for c in range(col_devs):
        for slot in range(c * key_pad + keys, (c + 1) * key_pad):
            x_all[slot] = jnp.zeros(x_all.shape[1:], jnp.float32)
    single = singles_ref[...]
    frame = frames_ref[...]
    own_slot = pl.ds(slot_of(me), rows)
    for t in range(CS // LANES):
        x_all[own_slot, t, :] = single[:, t * LANES : (t + 1) * LANES].astype(jnp.float32)
    x_all[own_slot, CS // LANES, :] = jnp.concatenate(
        [frame, jnp.zeros((rows, LANES - 12), jnp.float32)], 1
    )
    loads[0].wait()
    for i in range(pair_own.shape[0]):
        pair_own[i] = pair_raw[:, i, :]
    for i in range(rows):
        pair_all[i, col] = pair_own[col * rows + i]
    pl.semaphore_wait(barrier, plane)

    def x_copy(source, peer, send_index):
        number = number_of(source)
        slot = pl.ds(slot_of(number), rows)
        return pltpu.make_async_remote_copy(
            src_ref=x_all.at[slot],
            dst_ref=x_all.at[slot],
            send_sem=x_send.at[send_index],
            recv_sem=x_recv.at[number],
            device_id=peer,
            device_id_type=MESH,
        )

    def x_direct(step):
        peer = in_plane(step)
        return x_copy(here, peer, number_of(peer))

    def x_relay(source):
        return x_copy(source, partner_of(here), number_of(partner_of(source)))

    def p_copy(peer_col, sent_col, send_index, recv_index):
        return pltpu.make_async_remote_copy(
            src_ref=pair_own.at[pl.ds(peer_col * rows, rows)],
            dst_ref=pair_all.at[:, sent_col],
            send_sem=p_send.at[send_index],
            recv_sem=p_recv.at[recv_index],
            device_id=(row, peer_col),
            device_id_type=MESH,
        )

    def send_x(step, carry):
        x_direct(step).start()
        return carry

    def send_p(step, carry):
        p_copy(lax.rem(col + step, col_devs), col, step, col).start()
        return carry

    lax.fori_loop(1, plane, send_x, 0)
    x_relay(here).start()
    lax.fori_loop(1, col_devs, send_p, 0)

    scalar = H * CH
    loads[1].wait()
    projected = lax.dot_general(
        single, w_query_ref[...], NT, preferred_element_type=jnp.float32
    )
    q_points = moved_points(frame, projected[:, scalar:], H * PQ)
    q_feat = jnp.concatenate([projected[:, :scalar]] + q_points, 1)

    raw = heads_ref[...]
    gamma_row = jnp.maximum(raw, 0.0) + jnp.log(1.0 + jnp.exp(-jnp.abs(raw)))
    eye = lax.broadcasted_iota(jnp.int32, (HP, H), 0) == lax.broadcasted_iota(
        jnp.int32, (HP, H), 1
    )
    gamma = jnp.sum(jnp.where(eye, gamma_row, 0.0), axis=1, keepdims=True)
    weight = gamma * (math.sqrt(2.0 / (9.0 * PQ)) / 2.0)
    scalar_part = jnp.where(head_mask(scalar, 0, CH, scalar), 1.0 / math.sqrt(CH), 0.0)
    point_mask = head_mask(3 * H * PQ, 0, PQ, H * PQ)
    point_part = jnp.where(point_mask, 2.0 * weight, 0.0)
    square_part = jnp.where(point_mask, -weight, 0.0)
    q_scale = jnp.concatenate([scalar_part, point_part], 1)
    spread = jnp.concatenate(
        [
            jnp.concatenate([q_feat[i : i + 1] * q_scale, square_part], 1)
            for i in range(rows)
        ],
        0,
    )
    q_square = [
        jnp.sum(
            jnp.where(point_mask, q_feat[i : i + 1, scalar:] ** 2, 0.0), axis=1, keepdims=True
        )
        * weight
        for i in range(rows)
    ]
    bias_weights = w_bias_ref[...]

    def pass_on(step, carry):
        source = in_plane(plane - step)
        x_relay(source).wait_recv()
        x_relay(source).start()
        return carry

    def wait_x(step, carry):
        x_relay(partner_of(in_plane(plane - step))).wait_recv()
        return carry

    lax.fori_loop(1, plane, pass_on, 0)
    lax.fori_loop(0, plane, wait_x, 0)
    loads[2].wait()

    chunk = LANES if slots % LANES == 0 else slots

    def key_side(start):
        part = pl.ds(start, chunk)
        inputs = [x_all[part, t, :].astype(jnp.bfloat16) for t in range(CS // LANES)]
        held = x_all[part, CS // LANES, :].T
        values = lax.dot_general(
            w_keyval_ref[...],
            jnp.concatenate(inputs, 1),
            NT,
            preferred_element_type=jnp.float32,
        )
        first, second = 2 * scalar, 2 * scalar + 3 * H * PQ
        key_points = moved_columns(held, values[first:second], H * PQ)
        value_points = moved_columns(held, values[second:], H * PV)
        squares = [point * point for point in key_points]
        k_feat[:, part] = jnp.concatenate([values[:scalar]] + key_points + squares, 0)
        v_feat[:, part] = jnp.concatenate([values[scalar:first]] + value_points, 0)

    if chunk == slots:
        key_side(0)
    else:

        @pl.loop(0, slots // chunk)
        def _(index):
            key_side(pl.multiple_of(index * chunk, chunk))

    inner = dot_exact(spread, k_feat[...], NN)

    def wait_p(step, carry):
        source = lax.rem(col + col_devs - step, col_devs)
        p_copy(source, source, step, source).wait_recv()
        return carry

    lax.fori_loop(1, col_devs, wait_p, 0)

    place = lax.rem(lax.broadcasted_iota(jnp.int32, (HP, slots), 1), key_pad)
    bias_rows = jnp.concatenate([bias_weights, jnp.zeros((HP - H, CZ), jnp.float32)], 0)
    shares, pooled = [], []
    for i in range(rows):
        block = pair_all[i]
        if key_pad != keys:
            block = jnp.concatenate(
                [block, jnp.zeros((col_devs, key_pad - keys, CZ), jnp.float32)], 1
            )
        block = block.reshape(slots, CZ)
        bias = dot_exact(bias_rows, block, NT)
        logits = math.sqrt(1.0 / 3.0) * (inner[i * HP : (i + 1) * HP] + bias - q_square[i])
        if key_pad != keys:
            logits = jnp.where(place < keys, logits, -jnp.inf)
        exponent = jnp.exp(logits - jnp.max(logits, axis=1, keepdims=True))
        share = exponent / jnp.sum(exponent, axis=1, keepdims=True)
        shares.append(share)
        pooled.append(dot_exact(share, block, NN))

    gathered = dot_exact(jnp.concatenate(shares, 0), v_feat[...], NT)
    value_masks = [head_mask(scalar, 0, CH, scalar), head_mask(3 * H * PV, 0, PV, H * PV)]
    value_mask = jnp.concatenate([jnp.where(mask, 1.0, 0.0) for mask in value_masks], 1)
    kept = jnp.concatenate(
        [
            jnp.sum(
                gathered[i * HP : (i + 1) * HP] * value_mask,
                axis=0,
                keepdims=True,
            )
            for i in range(rows)
        ],
        0,
    )
    wide = H * PV
    relative = [
        kept[:, scalar + b * wide : scalar + (b + 1) * wide] - frame[:, 9 + b : 10 + b]
        for b in range(3)
    ]
    local = [
        frame[:, a : a + 1] * relative[0]
        + frame[:, 3 + a : 4 + a] * relative[1]
        + frame[:, 6 + a : 7 + a] * relative[2]
        for a in range(3)
    ]
    length = jnp.sqrt(local[0] ** 2 + local[1] ** 2 + local[2] ** 2 + 1.0)
    loads[3].wait()
    features = jnp.concatenate([kept[:, :scalar]] + local + [length], 1).astype(jnp.bfloat16)
    split = H * (CH + 4 * PV)
    total = jnp.dot(features, w_out_ref[0:split, :], preferred_element_type=jnp.float32)
    flat = jnp.concatenate(
        [
            jnp.concatenate([pooled[i][h : h + 1] for i in range(rows)], 0)
            for h in range(H)
        ],
        1,
    )
    high = flat.astype(jnp.bfloat16)
    rest = flat - high.astype(jnp.float32)
    middle = rest.astype(jnp.bfloat16)
    low = (rest - middle.astype(jnp.float32)).astype(jnp.bfloat16)
    w_pair = w_out_ref[split:, :]
    for piece in (low, middle, high):
        total = total + jnp.dot(piece, w_pair, preferred_element_type=jnp.float32)
    out_ref[...] = total

    def end_x(step, carry):
        x_direct(step).wait_send()
        x_relay(in_plane(step)).wait_send()
        return carry

    def end_p(step, carry):
        p_copy(lax.rem(col + step, col_devs), col, step, col).wait_send()
        return carry

    x_relay(here).wait_send()
    lax.fori_loop(1, plane, end_x, 0)
    lax.fori_loop(1, col_devs, end_p, 0)


def solution(mesh):
    sizes = (mesh.shape["row"], mesh.shape["col"])
    devices = sizes[0] * sizes[1]

    def body(singles, pair, frames, w_query, w_keyval, w_bias, head_weights, w_out):
        rows = singles.shape[0]
        keys = pair.shape[1]
        slots = sizes[1] * round_up(keys, 8)
        vmem = pl.BlockSpec(memory_space=pltpu.VMEM)
        hbm = pl.BlockSpec(memory_space=pl.ANY)
        return pl.pallas_call(
            functools.partial(kernel, sizes),
            out_shape=jax.ShapeDtypeStruct((rows, w_out.shape[1]), jnp.float32),
            in_specs=[vmem] * 4 + [hbm] * 4,
            out_specs=vmem,
            scratch_shapes=[
                pltpu.VMEM((slots, CS // LANES + 1, LANES), jnp.float32),
                pltpu.VMEM((keys, pair.shape[0], CZ), jnp.float32),
                pltpu.VMEM(pair.shape, jnp.float32),
                pltpu.VMEM((rows, sizes[1], keys, CZ), jnp.float32),
                pltpu.VMEM(w_query.shape[::-1], w_query.dtype),
                pltpu.VMEM(w_keyval.shape[::-1], w_keyval.dtype),
                pltpu.VMEM(w_out.shape, w_out.dtype),
                pltpu.VMEM((H * CH + 6 * H * PQ, slots), jnp.float32),
                pltpu.VMEM((H * CH + 3 * H * PV, slots), jnp.float32),
                pltpu.SemaphoreType.DMA((4,)),
                pltpu.SemaphoreType.DMA((devices,)),
                pltpu.SemaphoreType.DMA((devices,)),
                pltpu.SemaphoreType.DMA((sizes[1],)),
                pltpu.SemaphoreType.DMA((sizes[1],)),
            ],
            compiler_params=pltpu.CompilerParams(
                collective_id=0, has_side_effects=True, vmem_limit_bytes=60 * 2**20
            ),
        )(
            singles,
            frames,
            w_bias.T,
            head_weights.reshape(1, H),
            pair.transpose(1, 0, 2),
            w_query.T,
            w_keyval.T,
            w_out,
        )

    return jax.shard_map(
        body,
        mesh=mesh,
        in_specs=(
            P(("row", "col"), None),
            P("row", "col", None),
            P(("row", "col"), None),
            P(),
            P(),
            P(),
            P(),
            P(),
        ),
        out_specs=P(("row", "col"), None),
        check_vma=False,
    )
```

profile of v0, /device:TPU:6, one launch (start us, length us, event | category | flops | bytes accessed | tf_op | source)
XLA Modules:
  0.0 147.8 jit_solution(9781401822808184683)
XLA Ops:
  0.0 3.8 %copy.11 = f32[96,48,128]{2,0,1:T(8,128)} copy(f32[96,48,128]{2,1,0:T(8,128)} %param.9) | data formatting | bytes 4718592 | tf_op args[1]
  3.8 142.7 %shard_map.82 = f32[3,384]{1,0:T(4,128)} custom-call(bf16[3,384]{1,0:T(4,128)(2,1)} %singles_ref.1, f32[3,12]{1,0:T(4,128)} %frames_ref.1, f32[12,128]{1,0:T(8,128)} %bitcast.10, f32[1,12]{1,0:T(1,128)} %bitcast.11, f32[48,96,128]{2,1,0:T(8,128)} %bitcast.7, bf16[336,384]{1,0:T(8,128)(2,1)} %bitcast.9, bf16[816,384]{1,0:T(8,128)(2,1)} %bitcast.8, ...), custom_call_target="tpu_custom_call" | custom-call | tf_op jit(solution)/shard_map/pallas_call | solution.py:374
  146.5 1.3 copy.13
where the time goes:
time: 148 us
  Pallas kernels  143 us (97%)
  local copies, waits for them, and re-layouts  5.12 us (3%)
    pallas_call x1, Pallas kernels, body(): pl.pallas_call(functools.partial(kernel, sizes), out_shape=jax.ShapeDtype...  143 us
    unnamed x2, local copies, waits for them, and re-layouts  5.12 us

commit v1 on v0

v1 whole, which is shorter than its diff:
```python
import functools
import math

import jax
import jax.numpy as jnp
from jax import lax
from jax.experimental import pallas as pl
from jax.experimental.pallas import tpu as pltpu
from jax.sharding import PartitionSpec as P

CS = 384
CZ = 128
H = 12
CH = 16
PQ = 4
PV = 8

HP = 16
LANES = 128
SCALAR = H * CH
VALUE = SCALAR + 3 * H * PV
SPLIT = H * (CH + 4 * PV)
GROUP = 32
FEAT = H * GROUP
SCALE = math.sqrt(1.0 / 3.0)
MESH = pl.DeviceIdType.MESH
NT = (((1,), (1,)), ((), ()))
NN = (((1,), (0,)), ((), ()))
F32 = jnp.float32
BF16 = jnp.bfloat16


def dot(left, right, dims):
    return lax.dot_general(left, right, dims, preferred_element_type=F32)


def pieces(value, count):
    result = []
    for _ in range(count):
        piece = value.astype(BF16).astype(F32)
        result.append(piece)
        value = value - piece
    return result


def iota(shape, dim):
    return lax.broadcasted_iota(jnp.int32, shape, dim)


def moved_points(frame, local, width):
    parts = [local[:, b * width : (b + 1) * width] for b in range(3)]
    return [
        frame[:, 3 * a : 3 * a + 1] * parts[0]
        + frame[:, 3 * a + 1 : 3 * a + 2] * parts[1]
        + frame[:, 3 * a + 2 : 3 * a + 3] * parts[2]
        + frame[:, 9 + a : 10 + a]
        for a in range(3)
    ]


def value_head(lane):
    points = lax.rem(lane - SCALAR, H * PV) // PV
    head = jnp.where(lane < SCALAR, lane // CH, points)
    return jnp.where(lane < VALUE, head, -1)


def kernel(
    sizes,
    singles_ref,
    frames_ref,
    w_bias_ref,
    heads_ref,
    pair_hbm,
    w_query_hbm,
    w_keyval_hbm,
    w_out_hbm,
    out_ref,
    pair_ref,
    pair_hi,
    pair_lo,
    w_query_ref,
    w_keyval_ref,
    w_out_ref,
    q_all,
    k_own,
    v_own,
    k_all,
    v_all,
    bias_ref,
    attn_ref,
    pooled_ref,
    lse_all,
    point_own,
    point_all,
    part_own,
    part_all,
    load_sem,
    q_send,
    q_recv,
    k_send,
    k_recv,
    v_send,
    v_recv,
    l_send,
    l_recv,
    o_send,
    o_recv,
    p_send,
    p_recv,
):
    row_devs, col_devs = sizes
    rows = singles_ref.shape[0]
    queries, keys = pair_ref.shape[0], pair_ref.shape[1]
    owners = keys // rows
    row = lax.axis_index("row")
    col = lax.axis_index("col")

    loads = [
        pltpu.make_async_copy(w_query_hbm, w_query_ref, load_sem.at[0]),
        pltpu.make_async_copy(w_keyval_hbm, w_keyval_ref, load_sem.at[1]),
        pltpu.make_async_copy(pair_hbm, pair_ref, load_sem.at[2]),
        pltpu.make_async_copy(w_out_hbm, w_out_ref, load_sem.at[3]),
    ]
    for load in loads:
        load.start()

    me = row * col_devs + col
    key_col = me // owners
    key_slot = lax.rem(me, owners)
    own_keys = key_col == col

    def source_of(slot):
        index = col * owners + slot
        return (index // col_devs, lax.rem(index, col_devs))

    barrier = pltpu.get_barrier_semaphore()

    def greet(peer):
        pl.semaphore_signal(barrier, inc=1, device_id=peer, device_id_type=MESH)

    def greet_source(step, carry):
        slot = lax.rem(key_slot + step, owners)

        @pl.when(jnp.logical_not(jnp.logical_and(own_keys, slot == key_slot)))
        def _():
            greet(source_of(slot))

        return carry

    def greet_row(step, carry):
        greet((row, lax.rem(col + step, col_devs)))
        return carry

    lax.fori_loop(0, owners, greet_source, 0)
    lax.fori_loop(1, col_devs, greet_row, 0)

    single = singles_ref[...]
    frame = frames_ref[...]
    loads[0].wait()
    query_proj = dot(single, w_query_ref[...], NT)
    loads[1].wait()
    key_proj = dot(single, w_keyval_ref[...], NT)

    lane = iota((1, FEAT), 1)
    lane_head = lane // GROUP
    within = lax.rem(lane, GROUP)
    is_scalar = within < CH
    axis = (within - CH) // PQ
    is_point = jnp.logical_and(within >= CH, within < CH + 3 * PQ)
    point = lax.rem(within - CH, PQ)
    targets = [jnp.where(is_scalar, lane_head * CH + within, -1)]
    for b in range(3):
        column = SCALAR + b * H * PQ + lane_head * PQ + point
        targets.append(jnp.where(is_point, column, -1))
    target = jnp.concatenate(targets, 1)
    width = SCALAR + 3 * H * PQ
    place = jnp.where(iota((width, 4 * FEAT), 0) == target, 1.0, 0.0).astype(BF16)
    key_part = jnp.concatenate(
        [key_proj[:, :SCALAR], key_proj[:, 2 * SCALAR : 2 * SCALAR + 3 * H * PQ]], 1
    )
    both = jnp.concatenate(
        [query_proj, key_part, jnp.zeros((8 - 2 * rows, width), F32)], 0
    )
    placed = dot(jnp.concatenate(pieces(both, 3), 0).astype(BF16), place, NN)
    placed = placed[0:8] + placed[8:16] + placed[16:24]
    frame8 = jnp.concatenate([frame, frame, jnp.zeros((8 - 2 * rows, 12), F32)], 0)

    def by_axis(first, stride):
        return jnp.where(
            axis == 0,
            frame8[:, first : first + 1],
            jnp.where(
                axis == 1,
                frame8[:, first + stride : first + stride + 1],
                frame8[:, first + 2 * stride : first + 2 * stride + 1],
            ),
        )

    moved = by_axis(9, 1)
    for b in range(3):
        moved = moved + by_axis(b, 3) * placed[:, (b + 1) * FEAT : (b + 2) * FEAT]
    moved = jnp.where(is_point, moved, 0.0)
    same_head = iota((FEAT, FEAT), 0) // GROUP == iota((FEAT, FEAT), 1) // GROUP
    same_head = jnp.where(same_head, 1.0, 0.0).astype(BF16)
    squares = jnp.concatenate(pieces(moved * moved, 3), 0).astype(BF16)
    squares = dot(squares, same_head, NN)
    squares = squares[0:8] + squares[8:16] + squares[16:24]

    raw = heads_ref[...]
    gamma = jnp.maximum(raw, 0.0) + jnp.log(1.0 + jnp.exp(-jnp.abs(raw)))
    weight = jnp.zeros((1, FEAT), F32)
    for h in range(H):
        weight = jnp.where(lane_head == h, gamma[:, h : h + 1], weight)
    weight = weight * (SCALE * math.sqrt(2.0 / (9.0 * PQ)) / 2.0)
    scalars = placed[:, :FEAT]
    first_extra = within == CH + 3 * PQ
    second_extra = within == CH + 3 * PQ + 1
    zero = jnp.zeros((8, FEAT), F32)
    q_feat = jnp.where(is_scalar, scalars * (SCALE / math.sqrt(CH)), moved * (2.0 * weight))
    q_feat = jnp.where(first_extra, -weight * squares, q_feat)
    q_feat = jnp.where(second_extra, weight + zero, q_feat)
    k_feat = jnp.where(is_scalar, scalars, moved)
    k_feat = jnp.where(first_extra, 1.0, k_feat)
    k_feat = jnp.where(second_extra, -squares, k_feat)
    v_points = moved_points(frame, key_proj[:, 2 * SCALAR + 3 * H * PQ :], H * PV)
    v_feat = jnp.concatenate(
        [key_proj[:, SCALAR : 2 * SCALAR]]
        + v_points
        + [jnp.zeros((rows, 4 * LANES - VALUE), F32)],
        1,
    )

    own_rows = pl.ds(col * rows, rows)
    key_rows = pl.ds(key_slot * rows, rows)
    for t in range(FEAT // LANES):
        part = slice(t * LANES, (t + 1) * LANES)
        q_all[own_rows, t, :] = q_feat[0:rows, part]
        k_own[:, t, :] = k_feat[rows : 2 * rows, part]
    for t in range(4):
        v_own[:, t, :] = v_feat[:, t * LANES : (t + 1) * LANES]

    @pl.when(own_keys)
    def _():
        for t in range(FEAT // LANES):
            k_all[key_rows, t, :] = k_feat[rows : 2 * rows, t * LANES : (t + 1) * LANES]
        for t in range(4):
            v_all[key_rows, t, :] = v_feat[:, t * LANES : (t + 1) * LANES]

    pl.semaphore_wait(barrier, owners + col_devs - 1 - own_keys.astype(jnp.int32))

    def key_copy(src, dst, peer, slot, send, recv, index):
        return pltpu.make_async_remote_copy(
            src_ref=src,
            dst_ref=dst.at[pl.ds(slot * rows, rows)],
            send_sem=send.at[index],
            recv_sem=recv.at[slot],
            device_id=peer,
            device_id_type=MESH,
        )

    def k_copy(peer, slot, index):
        return key_copy(k_own, k_all, peer, slot, k_send, k_recv, index)

    def v_copy(peer, slot, index):
        return key_copy(v_own, v_all, peer, slot, v_send, v_recv, index)

    def each_key_peer(act):
        def body(step, carry):
            peer_row = lax.rem(row + step, row_devs)

            @pl.when(jnp.logical_not(jnp.logical_and(own_keys, peer_row == row)))
            def _():
                act((peer_row, key_col), step)

            return carry

        lax.fori_loop(0, row_devs, body, 0)

    def each_source(act):
        def body(slot, carry):
            @pl.when(jnp.logical_not(jnp.logical_and(own_keys, slot == key_slot)))
            def _():
                act(source_of(slot), slot)

            return carry

        lax.fori_loop(0, owners, body, 0)

    def each_row_peer(act):
        def body(step, carry):
            act(lax.rem(col + step, col_devs), step)
            return carry

        lax.fori_loop(1, col_devs, body, 0)

    def row_copy(src, dst, peer, source, send, recv, index):
        return pltpu.make_async_remote_copy(
            src_ref=src,
            dst_ref=dst,
            send_sem=send.at[index],
            recv_sem=recv.at[source],
            device_id=(row, peer),
            device_id_type=MESH,
        )

    def q_copy(peer, source, index):
        at = pl.ds(source * rows, rows)
        return row_copy(q_all.at[at], q_all.at[at], peer, source, q_send, q_recv, index)

    def l_copy(peer, source, index):
        return row_copy(
            lse_all.at[source], lse_all.at[source], peer, source, l_send, l_recv, index
        )

    def o_copy(peer, source, index):
        return row_copy(
            point_own.at[pl.ds(peer * rows, rows)],
            point_all.at[source],
            peer,
            source,
            o_send,
            o_recv,
            index,
        )

    def p_copy(peer, source, index):
        return row_copy(
            part_own.at[pl.ds(peer * rows, rows)],
            part_all.at[source],
            peer,
            source,
            p_send,
            p_recv,
            index,
        )

    each_key_peer(lambda peer, step: k_copy(peer, key_slot, step).start())
    each_row_peer(lambda peer, step: q_copy(peer, col, step).start())
    each_key_peer(lambda peer, step: v_copy(peer, key_slot, step).start())

    bias_rows = jnp.concatenate([w_bias_ref[...] * SCALE, jnp.zeros((HP - H, CZ), F32)], 0)
    bias_pieces = jnp.concatenate(pieces(bias_rows, 3), 0).astype(BF16)
    loads[2].wait()

    @pl.loop(0, queries // 4)
    def _(block):
        for u in range(4):
            i = block * 4 + u
            high, middle, low = [piece.astype(BF16) for piece in pieces(pair_ref[i], 3)]
            pair_hi[i] = high
            pair_lo[i] = middle
            first = dot(bias_pieces, high, NT)
            second = dot(bias_pieces[0 : 2 * HP], middle, NT)
            third = dot(bias_pieces[0:HP], low, NT)
            small = first[2 * HP :] + second[HP:] + third
            bias_ref[i] = first[0:HP] + (first[HP : 2 * HP] + second[0:HP] + small)

    each_source(lambda peer, slot: k_copy(peer, slot, slot).wait_recv())
    each_row_peer(lambda peer, step: q_copy(peer, peer, step).wait_recv())

    lse_lane = VALUE % LANES
    lane128 = iota((1, LANES), 1)
    lse = jnp.zeros((queries, LANES), F32)
    for t in range(FEAT // LANES):
        q1, q2, q3 = [piece.astype(BF16) for piece in pieces(q_all[:, t, :], 3)]
        k1, k2, k3 = [piece.astype(BF16) for piece in pieces(k_all[:, t, :], 3)]
        left = jnp.concatenate([q1, q1, q2, q1, q2, q3], 1)
        right = jnp.concatenate([k1, k2, k1, k3, k2, k1], 1)
        tile_head = lax.rem(iota((1, 6 * LANES), 1), LANES) // GROUP
        for g in range(LANES // GROUP):
            h = t * (LANES // GROUP) + g
            mask = jnp.where(tile_head == g, 1.0, 0.0).astype(BF16)
            logits = dot(left, right * mask, NT) + bias_ref[:, h, :]
            top = jnp.max(logits, axis=1, keepdims=True)
            exponent = jnp.exp(logits - top)
            total = jnp.sum(exponent, axis=1, keepdims=True)
            attn_ref[:, h, :] = exponent * (1.0 / total)
            lse = jnp.where(lane128 == lse_lane + h, top + jnp.log(total), lse)

    turned = jnp.concatenate([lse, jnp.zeros((LANES - queries, LANES), F32)], 0).T
    own_lse = turned[lse_lane : lse_lane + HP]
    lse_all[col] = own_lse
    each_row_peer(lambda peer, step: l_copy(peer, col, step).start())

    each_source(lambda peer, slot: v_copy(peer, slot, slot).wait_recv())
    values = jnp.concatenate([v_all[:, t, :] for t in range(4)], 1)
    v1, v2 = [piece.astype(BF16) for piece in pieces(values, 2)]
    lane_of = value_head(iota((1, 4 * LANES), 1))
    gathered = jnp.zeros((queries, 4 * LANES), F32)
    for h in range(H):
        mask = jnp.where(lane_of == h, 1.0, 0.0).astype(BF16)
        a1, a2 = [piece.astype(BF16) for piece in pieces(attn_ref[:, h, :], 2)]
        left = jnp.concatenate([a1, a2], 0)
        high = dot(left, v1 * mask, NN)
        low = dot(a1, v2 * mask, NN)
        gathered = gathered + (high[0:queries] + (high[queries:] + low))
    for t in range(4):
        tile = gathered[:, t * LANES : (t + 1) * LANES]
        if t == 3:
            tile = jnp.where(lane128 >= lse_lane, lse, tile)
        point_own[:, t, :] = tile
    for i in range(rows):
        point_all[col, i] = point_own[col * rows + i]
    each_row_peer(lambda peer, step: o_copy(peer, col, step).start())

    @pl.loop(0, queries // 4)
    def _(block):
        for u in range(4):
            i = block * 4 + u
            stacked = jnp.concatenate(pieces(attn_ref[i], 2), 0).astype(BF16)
            high = dot(stacked, pair_hi[i], NN)
            low = dot(stacked[0:HP], pair_lo[i], NN)
            pooled_ref[i] = high[0:HP] + (high[HP:] + low)

    loads[3].wait()
    each_row_peer(lambda peer, step: l_copy(peer, peer, step).wait_recv())
    everyone = lse_all[...]
    top = jnp.max(everyone, axis=0)
    whole = top + jnp.log(jnp.sum(jnp.exp(everyone - top[None]), axis=0))
    factor = jnp.exp(own_lse - whole)
    factor = jnp.concatenate([factor, jnp.zeros((LANES - HP, LANES), F32)], 0).T
    projected = jnp.zeros((queries, CS), F32)
    for h in range(0, H, 2):
        scaled = jnp.concatenate(
            [pooled_ref[:, g, :] * factor[0:queries, g : g + 1] for g in (h, h + 1)], 1
        )
        stacked = jnp.concatenate(pieces(scaled, 2), 0).astype(BF16)
        share = dot(stacked, w_out_ref[SPLIT + h * CZ : SPLIT + (h + 2) * CZ, :], NN)
        projected = projected + (share[0:queries] + share[queries:])
    for t in range(CS // LANES):
        part_own[:, t, :] = projected[:, t * LANES : (t + 1) * LANES]
    for i in range(rows):
        part_all[col, i] = part_own[col * rows + i]
    each_row_peer(lambda peer, step: p_copy(peer, col, step).start())

    each_row_peer(lambda peer, step: o_copy(peer, peer, step).wait_recv())
    shares = []
    for i in range(rows):
        sums = point_all[:, i, 3, :]
        share = jnp.exp(sums - jnp.max(sums, axis=0, keepdims=True))
        share = share / jnp.sum(share, axis=0, keepdims=True)
        shares.append(share)
    shares = jnp.concatenate(pieces(jnp.concatenate(shares, 0), 2), 0).astype(BF16)
    spread = iota((LANES, 4 * LANES), 0) - lse_lane == value_head(
        iota((LANES, 4 * LANES), 1)
    )
    spread = jnp.logical_and(spread, iota((LANES, 4 * LANES), 0) >= lse_lane)
    wide = dot(shares, jnp.where(spread, 1.0, 0.0).astype(BF16), NN)
    count = rows * col_devs
    wide = wide[0:count] + wide[count:]
    kept = jnp.concatenate(
        [
            jnp.concatenate(
                [
                    jnp.sum(
                        point_all[:, i, t, :]
                        * wide[
                            i * col_devs : (i + 1) * col_devs, t * LANES : (t + 1) * LANES
                        ],
                        axis=0,
                        keepdims=True,
                    )
                    for t in range(4)
                ],
                1,
            )
            for i in range(rows)
        ],
        0,
    )
    wide = H * PV
    relative = [
        kept[:, SCALAR + b * wide : SCALAR + (b + 1) * wide] - frame[:, 9 + b : 10 + b]
        for b in range(3)
    ]
    local = [
        frame[:, a : a + 1] * relative[0]
        + frame[:, 3 + a : 4 + a] * relative[1]
        + frame[:, 6 + a : 7 + a] * relative[2]
        for a in range(3)
    ]
    length = jnp.sqrt(local[0] ** 2 + local[1] ** 2 + local[2] ** 2 + 1.0)
    features = jnp.concatenate([kept[:, :SCALAR]] + local + [length], 1).astype(BF16)
    update = dot(features, w_out_ref[0:SPLIT, :], NN)

    each_row_peer(lambda peer, step: p_copy(peer, peer, step).wait_recv())
    for t in range(CS // LANES):
        part = slice(t * LANES, (t + 1) * LANES)
        terms = [
            jnp.sum(part_all[:, i, t, :], axis=0, keepdims=True) for i in range(rows)
        ]
        out_ref[:, part] = update[:, part] + jnp.concatenate(terms, 0)

    each_key_peer(lambda peer, step: k_copy(peer, key_slot, step).wait_send())
    each_key_peer(lambda peer, step: v_copy(peer, key_slot, step).wait_send())
    each_row_peer(lambda peer, step: q_copy(peer, col, step).wait_send())
    each_row_peer(lambda peer, step: l_copy(peer, col, step).wait_send())
    each_row_peer(lambda peer, step: o_copy(peer, col, step).wait_send())
    each_row_peer(lambda peer, step: p_copy(peer, col, step).wait_send())


def solution(mesh):
    sizes = (mesh.shape["row"], mesh.shape["col"])

    def body(singles, pair, frames, w_query, w_keyval, w_bias, head_weights, w_out):
        rows = singles.shape[0]
        queries, keys = pair.shape[0], pair.shape[1]
        owners = keys // rows
        vmem = pl.BlockSpec(memory_space=pltpu.VMEM)
        hbm = pl.BlockSpec(memory_space=pl.ANY)
        dma = pltpu.SemaphoreType.DMA
        return pl.pallas_call(
            functools.partial(kernel, sizes),
            out_shape=jax.ShapeDtypeStruct((rows, w_out.shape[1]), F32),
            in_specs=[vmem] * 4 + [hbm] * 4,
            out_specs=vmem,
            scratch_shapes=[
                pltpu.VMEM(pair.shape, F32),
                pltpu.VMEM(pair.shape, BF16),
                pltpu.VMEM(pair.shape, BF16),
                pltpu.VMEM(w_query.shape[::-1], w_query.dtype),
                pltpu.VMEM(w_keyval.shape[::-1], w_keyval.dtype),
                pltpu.VMEM(w_out.shape, w_out.dtype),
                pltpu.VMEM((queries, FEAT // LANES, LANES), F32),
                pltpu.VMEM((rows, FEAT // LANES, LANES), F32),
                pltpu.VMEM((rows, 4, LANES), F32),
                pltpu.VMEM((keys, FEAT // LANES, LANES), F32),
                pltpu.VMEM((keys, 4, LANES), F32),
                pltpu.VMEM((queries, HP, keys), F32),
                pltpu.VMEM((queries, HP, keys), F32),
                pltpu.VMEM((queries, HP, CZ), F32),
                pltpu.VMEM((sizes[1], HP, LANES), F32),
                pltpu.VMEM((queries, 4, LANES), F32),
                pltpu.VMEM((sizes[1], rows, 4, LANES), F32),
                pltpu.VMEM((queries, CS // LANES, LANES), F32),
                pltpu.VMEM((sizes[1], rows, CS // LANES, LANES), F32),
                dma((4,)),
                dma((sizes[1],)),
                dma((sizes[1],)),
                dma((sizes[0],)),
                dma((owners,)),
                dma((sizes[0],)),
                dma((owners,)),
                dma((sizes[1],)),
                dma((sizes[1],)),
                dma((sizes[1],)),
                dma((sizes[1],)),
                dma((sizes[1],)),
                dma((sizes[1],)),
            ],
            compiler_params=pltpu.CompilerParams(
                collective_id=0, has_side_effects=True, vmem_limit_bytes=60 * 2**20
            ),
        )(
            singles,
            frames,
            w_bias.T,
            head_weights.reshape(1, H),
            pair,
            w_query.T,
            w_keyval.T,
            w_out,
        )

    return jax.shard_map(
        body,
        mesh=mesh,
        in_specs=(
            P(("row", "col"), None),
            P("row", "col", None),
            P(("row", "col"), None),
            P(),
            P(),
            P(),
            P(),
            P(),
        ),
        out_specs=P(("row", "col"), None),
        check_vma=False,
    )
```

time: 148 us -> 52.6 us (0.36)
  the two profiles are of different devices: /device:TPU:6 before, /device:TPU:56 now
where the time goes in v1:
time: 52.6 us; the launch traced here: 52.4 us
  Pallas kernels  51.1 us (97%)
  local copies, waits for them, and re-layouts  1.29 us (2%)
    pallas_call x1, Pallas kernels, body(): pl.pallas_call(functools.partial(kernel, sizes), out_shape=jax.ShapeDtype...  51.1 us
    unnamed x1, local copies, waits for them, and re-layouts  1.29 us

profile of v1, /device:TPU:56, one launch (start us, length us, event | category | flops | bytes accessed | tf_op | source)
XLA Modules:
  0.0 52.4 jit_solution(6219252832321459487)
XLA Ops:
  0.0 51.1 %shard_map.82 = f32[3,384]{1,0:T(4,128)} custom-call(bf16[3,384]{1,0:T(4,128)(2,1)} %singles_ref.1, f32[3,12]{1,0:T(4,128)} %frames_ref.1, f32[12,128]{1,0:T(8,128)} %bitcast.6, f32[1,12]{1,0:T(1,128)} %bitcast.7, f32[96,48,128]{2,1,0:T(8,128)} %pair_hbm.1, bf16[336,384]{1,0:T(8,128)(2,1)} %bitcast.5, bf16[816,384]{1,0:T(8,128)(2,1)} %bitcast.4, ...), custom_call_target="tpu_custom_call" | custom-call | tf_op jit(solution)/shard_map/pallas_call | solution.py:512
  51.1 1.3 %copy.10 = f32[3,384]{1,0:T(4,128)} copy(f32[3,384]{1,0:T(4,128)} %shard_map.82) | data formatting | bytes 9216

commit v2 on v1

--- a/solution.py
+++ b/solution.py
@@ -21,6 +21,7 @@
 VALUE = SCALAR + 3 * H * PV
 SPLIT = H * (CH + 4 * PV)
 GROUP = 32
+INNER = 4
 FEAT = H * GROUP
 SCALE = math.sqrt(1.0 / 3.0)
 MESH = pl.DeviceIdType.MESH
@@ -58,6 +59,11 @@
     ]
 
 
+def merged(sums):
+    top = jnp.max(sums, axis=0)
+    return top + jnp.log(jnp.sum(jnp.exp(sums - top[None]), axis=0))
+
+
 def value_head(lane):
     points = lax.rem(lane - SCALAR, H * PV) // PV
     head = jnp.where(lane < SCALAR, lane // CH, points)
@@ -66,15 +72,19 @@
 
 def kernel(
     sizes,
-    singles_ref,
-    frames_ref,
-    w_bias_ref,
-    heads_ref,
+    singles_hbm,
+    frames_hbm,
+    w_bias_hbm,
+    heads_hbm,
     pair_hbm,
     w_query_hbm,
     w_keyval_hbm,
     w_out_hbm,
     out_ref,
+    singles_ref,
+    frames_ref,
+    w_bias_ref,
+    heads_ref,
     pair_ref,
     pair_hi,
     pair_lo,
@@ -89,24 +99,15 @@
     bias_ref,
     attn_ref,
     pooled_ref,
-    lse_all,
+    lse_inner,
+    lse_outer,
     point_own,
     point_all,
     part_own,
     part_all,
     load_sem,
-    q_send,
-    q_recv,
-    k_send,
-    k_recv,
-    v_send,
-    v_recv,
-    l_send,
-    l_recv,
-    o_send,
-    o_recv,
-    p_send,
-    p_recv,
+    send_sem,
+    recv_sem,
 ):
     row_devs, col_devs = sizes
     rows = singles_ref.shape[0]
@@ -115,19 +116,16 @@
     row = lax.axis_index("row")
     col = lax.axis_index("col")
 
-    loads = [
-        pltpu.make_async_copy(w_query_hbm, w_query_ref, load_sem.at[0]),
-        pltpu.make_async_copy(w_keyval_hbm, w_keyval_ref, load_sem.at[1]),
-        pltpu.make_async_copy(pair_hbm, pair_ref, load_sem.at[2]),
-        pltpu.make_async_copy(w_out_hbm, w_out_ref, load_sem.at[3]),
-    ]
-    for load in loads:
-        load.start()
-
     me = row * col_devs + col
     key_col = me // owners
     key_slot = lax.rem(me, owners)
     own_keys = key_col == col
+    core = lax.rem(row, 2)
+    partner = (row + 1 - 2 * core, col)
+    inner_devs = INNER
+    outer_devs = col_devs // INNER
+    inner = lax.rem(col, INNER)
+    outer = col // INNER
 
     def source_of(slot):
         index = col * owners + slot
@@ -153,13 +151,32 @@
 
     lax.fori_loop(0, owners, greet_source, 0)
     lax.fori_loop(1, col_devs, greet_row, 0)
-
+    greet(partner)
+
+    moves = [
+        (singles_hbm, singles_ref),
+        (w_query_hbm, w_query_ref),
+        (w_keyval_hbm, w_keyval_ref),
+        (frames_hbm, frames_ref),
+        (heads_hbm, heads_ref),
+        (w_bias_hbm, w_bias_ref),
+        (pair_hbm, pair_ref),
+        (w_out_hbm, w_out_ref),
+    ]
+    loads = [
+        pltpu.make_async_copy(src, dst, load_sem.at[n]) for n, (src, dst) in enumerate(moves)
+    ]
+    for load in loads:
+        load.start()
+
+    loads[0].wait()
     single = singles_ref[...]
+    loads[1].wait()
+    query_proj = dot(single, w_query_ref[...], NT)
+    loads[2].wait()
+    key_proj = dot(single, w_keyval_ref[...], NT)
+    loads[3].wait()
     frame = frames_ref[...]
-    loads[0].wait()
-    query_proj = dot(single, w_query_ref[...], NT)
-    loads[1].wait()
-    key_proj = dot(single, w_keyval_ref[...], NT)
 
     lane = iota((1, FEAT), 1)
     lane_head = lane // GROUP
@@ -206,6 +223,7 @@
     squares = dot(squares, same_head, NN)
     squares = squares[0:8] + squares[8:16] + squares[16:24]
 
+    loads[4].wait()
     raw = heads_ref[...]
     gamma = jnp.maximum(raw, 0.0) + jnp.log(1.0 + jnp.exp(-jnp.abs(raw)))
     weight = jnp.zeros((1, FEAT), F32)
@@ -246,106 +264,69 @@
         for t in range(4):
             v_all[key_rows, t, :] = v_feat[:, t * LANES : (t + 1) * LANES]
 
-    pl.semaphore_wait(barrier, owners + col_devs - 1 - own_keys.astype(jnp.int32))
-
-    def key_copy(src, dst, peer, slot, send, recv, index):
+    pl.semaphore_wait(barrier, owners + col_devs - own_keys.astype(jnp.int32))
+
+    def remote(src, dst, peer, kind):
         return pltpu.make_async_remote_copy(
             src_ref=src,
-            dst_ref=dst.at[pl.ds(slot * rows, rows)],
-            send_sem=send.at[index],
-            recv_sem=recv.at[slot],
+            dst_ref=dst,
+            send_sem=send_sem.at[kind],
+            recv_sem=recv_sem.at[kind],
             device_id=peer,
             device_id_type=MESH,
         )
 
-    def k_copy(peer, slot, index):
-        return key_copy(k_own, k_all, peer, slot, k_send, k_recv, index)
-
-    def v_copy(peer, slot, index):
-        return key_copy(v_own, v_all, peer, slot, v_send, v_recv, index)
-
-    def each_key_peer(act):
-        def body(step, carry):
-            peer_row = lax.rem(row + step, row_devs)
+    def sent(ref, kind):
+        remote(ref, ref, partner, kind).wait_send()
+
+    def received(ref, kind):
+        remote(ref, ref, partner, kind).wait_recv()
+
+    def of_others(act, ref, count, kind):
+        @pl.when(own_keys)
+        def _():
+            act(ref.at[pl.ds(0, (count - 1) * rows)], kind)
+
+        @pl.when(jnp.logical_not(own_keys))
+        def _():
+            act(ref.at[pl.ds(0, count * rows)], kind)
+
+    K, Q, V, RELAY, LSE_INNER, LSE_OUTER, POINT, PART = range(8)
+
+    def each_key_peer(first, step, act):
+        def body(n, carry):
+            peer_row = lax.rem(row + n * step + first, row_devs)
 
             @pl.when(jnp.logical_not(jnp.logical_and(own_keys, peer_row == row)))
             def _():
-                act((peer_row, key_col), step)
+                act((peer_row, key_col))
 
             return carry
 
-        lax.fori_loop(0, row_devs, body, 0)
-
-    def each_source(act):
-        def body(slot, carry):
-            @pl.when(jnp.logical_not(jnp.logical_and(own_keys, slot == key_slot)))
-            def _():
-                act(source_of(slot), slot)
-
-            return carry
-
-        lax.fori_loop(0, owners, body, 0)
+        lax.fori_loop(0, row_devs // step, body, 0)
 
     def each_row_peer(act):
         def body(step, carry):
-            act(lax.rem(col + step, col_devs), step)
+            act(lax.rem(col + step, col_devs))
             return carry
 
         lax.fori_loop(1, col_devs, body, 0)
 
-    def row_copy(src, dst, peer, source, send, recv, index):
-        return pltpu.make_async_remote_copy(
-            src_ref=src,
-            dst_ref=dst,
-            send_sem=send.at[index],
-            recv_sem=recv.at[source],
-            device_id=(row, peer),
-            device_id_type=MESH,
-        )
-
-    def q_copy(peer, source, index):
-        at = pl.ds(source * rows, rows)
-        return row_copy(q_all.at[at], q_all.at[at], peer, source, q_send, q_recv, index)
-
-    def l_copy(peer, source, index):
-        return row_copy(
-            lse_all.at[source], lse_all.at[source], peer, source, l_send, l_recv, index
-        )
-
-    def o_copy(peer, source, index):
-        return row_copy(
-            point_own.at[pl.ds(peer * rows, rows)],
-            point_all.at[source],
-            peer,
-            source,
-            o_send,
-            o_recv,
-            index,
-        )
-
-    def p_copy(peer, source, index):
-        return row_copy(
-            part_own.at[pl.ds(peer * rows, rows)],
-            part_all.at[source],
-            peer,
-            source,
-            p_send,
-            p_recv,
-            index,
-        )
-
-    each_key_peer(lambda peer, step: k_copy(peer, key_slot, step).start())
-    each_row_peer(lambda peer, step: q_copy(peer, col, step).start())
-    each_key_peer(lambda peer, step: v_copy(peer, key_slot, step).start())
-
+    key_rows = pl.ds(key_slot * rows, rows)
+    peers = col_devs - 1
+    each_key_peer(0, 1, lambda peer: remote(k_own, k_all.at[key_rows], peer, K).start())
+    each_row_peer(
+        lambda peer: remote(q_all.at[own_rows], q_all.at[own_rows], (row, peer), Q).start()
+    )
+
+    loads[5].wait()
     bias_rows = jnp.concatenate([w_bias_ref[...] * SCALE, jnp.zeros((HP - H, CZ), F32)], 0)
     bias_pieces = jnp.concatenate(pieces(bias_rows, 3), 0).astype(BF16)
-    loads[2].wait()
-
-    @pl.loop(0, queries // 4)
-    def _(block):
-        for u in range(4):
-            i = block * 4 + u
+    loads[6].wait()
+
+    def bias_block(block):
+        for u in range(8):
+            i = block * 8 + u
             high, middle, low = [piece.astype(BF16) for piece in pieces(pair_ref[i], 3)]
             pair_hi[i] = high
             pair_lo[i] = middle
@@ -355,8 +336,13 @@
             small = first[2 * HP :] + second[HP:] + third
             bias_ref[i] = first[0:HP] + (first[HP : 2 * HP] + second[0:HP] + small)
 
-    each_source(lambda peer, slot: k_copy(peer, slot, slot).wait_recv())
-    each_row_peer(lambda peer, step: q_copy(peer, peer, step).wait_recv())
+    blocks = queries // 8
+    pl.loop(0, blocks // 2)(bias_block)
+    each_key_peer(0, 2, lambda peer: remote(v_own, v_all.at[key_rows], peer, V).start())
+    pl.loop(blocks // 2, blocks)(bias_block)
+
+    of_others(received, k_all, owners, K)
+    received(q_all.at[pl.ds(0, peers * rows)], Q)
 
     lse_lane = VALUE % LANES
     lane128 = iota((1, LANES), 1)
@@ -379,10 +365,23 @@
 
     turned = jnp.concatenate([lse, jnp.zeros((LANES - queries, LANES), F32)], 0).T
     own_lse = turned[lse_lane : lse_lane + HP]
-    lse_all[col] = own_lse
-    each_row_peer(lambda peer, step: l_copy(peer, col, step).start())
-
-    each_source(lambda peer, slot: v_copy(peer, slot, slot).wait_recv())
+    lse_inner[inner] = own_lse
+    for step in range(1, inner_devs):
+        peer = outer * inner_devs + lax.rem(inner + step, inner_devs)
+        slot = lse_inner.at[inner]
+        remote(slot, slot, (row, peer), LSE_INNER).start()
+
+    direct = lax.rem(col // 2, 2) == core
+
+    @pl.when(direct)
+    def _():
+        of_others(received, v_all, owners, V)
+        remote(v_all, v_all, partner, RELAY).start()
+
+    @pl.when(jnp.logical_not(direct))
+    def _():
+        received(v_all, RELAY)
+
     values = jnp.concatenate([v_all[:, t, :] for t in range(4)], 1)
     v1, v2 = [piece.astype(BF16) for piece in pieces(values, 2)]
     lane_of = value_head(iota((1, 4 * LANES), 1))
@@ -401,23 +400,32 @@
         point_own[:, t, :] = tile
     for i in range(rows):
         point_all[col, i] = point_own[col * rows + i]
-    each_row_peer(lambda peer, step: o_copy(peer, col, step).start())
-
-    @pl.loop(0, queries // 4)
+
+    received(lse_inner.at[pl.ds(0, inner_devs - 1)], LSE_INNER)
+    lse_outer[outer] = merged(lse_inner[...])
+    for step in range(1, outer_devs):
+        peer = lax.rem(outer + step, outer_devs) * inner_devs + inner
+        slot = lse_outer.at[outer]
+        remote(slot, slot, (row, peer), LSE_OUTER).start()
+
+    def send_points(peer):
+        theirs = point_own.at[pl.ds(peer * rows, rows)]
+        remote(theirs, point_all.at[col], (row, peer), POINT).start()
+
+    each_row_peer(send_points)
+
+    @pl.loop(0, queries // 8)
     def _(block):
-        for u in range(4):
-            i = block * 4 + u
+        for u in range(8):
+            i = block * 8 + u
             stacked = jnp.concatenate(pieces(attn_ref[i], 2), 0).astype(BF16)
             high = dot(stacked, pair_hi[i], NN)
             low = dot(stacked[0:HP], pair_lo[i], NN)
             pooled_ref[i] = high[0:HP] + (high[HP:] + low)
 
-    loads[3].wait()
-    each_row_peer(lambda peer, step: l_copy(peer, peer, step).wait_recv())
-    everyone = lse_all[...]
-    top = jnp.max(everyone, axis=0)
-    whole = top + jnp.log(jnp.sum(jnp.exp(everyone - top[None]), axis=0))
-    factor = jnp.exp(own_lse - whole)
+    loads[7].wait()
+    received(lse_outer.at[pl.ds(0, outer_devs - 1)], LSE_OUTER)
+    factor = jnp.exp(own_lse - merged(lse_outer[...]))
     factor = jnp.concatenate([factor, jnp.zeros((LANES - HP, LANES), F32)], 0).T
     projected = jnp.zeros((queries, CS), F32)
     for h in range(0, H, 2):
@@ -431,9 +439,14 @@
         part_own[:, t, :] = projected[:, t * LANES : (t + 1) * LANES]
     for i in range(rows):
         part_all[col, i] = part_own[col * rows + i]
-    each_row_peer(lambda peer, step: p_copy(peer, col, step).start())
-
-    each_row_peer(lambda peer, step: o_copy(peer, peer, step).wait_recv())
+
+    def send_part(peer):
+        theirs = part_own.at[pl.ds(peer * rows, rows)]
+        remote(theirs, part_all.at[col], (row, peer), PART).start()
+
+    each_row_peer(send_part)
+
+    received(point_all.at[pl.ds(0, peers)], POINT)
     shares = []
     for i in range(rows):
         sums = point_all[:, i, 3, :]
@@ -483,7 +496,7 @@
     features = jnp.concatenate([kept[:, :SCALAR]] + local + [length], 1).astype(BF16)
     update = dot(features, w_out_ref[0:SPLIT, :], NN)
 
-    each_row_peer(lambda peer, step: p_copy(peer, peer, step).wait_recv())
+    received(part_all.at[pl.ds(0, peers)], PART)
     for t in range(CS // LANES):
         part = slice(t * LANES, (t + 1) * LANES)
         terms = [
@@ -491,12 +504,18 @@
         ]
         out_ref[:, part] = update[:, part] + jnp.concatenate(terms, 0)
 
-    each_key_peer(lambda peer, step: k_copy(peer, key_slot, step).wait_send())
-    each_key_peer(lambda peer, step: v_copy(peer, key_slot, step).wait_send())
-    each_row_peer(lambda peer, step: q_copy(peer, col, step).wait_send())
-    each_row_peer(lambda peer, step: l_copy(peer, col, step).wait_send())
-    each_row_peer(lambda peer, step: o_copy(peer, col, step).wait_send())
-    each_row_peer(lambda peer, step: p_copy(peer, col, step).wait_send())
+    of_others(sent, k_all, row_devs, K)
+    of_others(sent, v_all, row_devs // 2, V)
+
+    @pl.when(direct)
+    def _():
+        sent(v_all, RELAY)
+
+    sent(q_all.at[pl.ds(0, peers * rows)], Q)
+    sent(lse_inner.at[pl.ds(0, inner_devs - 1)], LSE_INNER)
+    sent(lse_outer.at[pl.ds(0, outer_devs - 1)], LSE_OUTER)
+    sent(point_own.at[pl.ds(0, peers * rows)], POINT)
+    sent(part_own.at[pl.ds(0, peers * rows)], PART)
 
 
 def solution(mesh):
@@ -512,9 +531,13 @@
         return pl.pallas_call(
             functools.partial(kernel, sizes),
             out_shape=jax.ShapeDtypeStruct((rows, w_out.shape[1]), F32),
-            in_specs=[vmem] * 4 + [hbm] * 4,
+            in_specs=[hbm] * 8,
             out_specs=vmem,
             scratch_shapes=[
+                pltpu.VMEM(singles.shape, singles.dtype),
+                pltpu.VMEM(frames.shape, F32),
+                pltpu.VMEM(w_bias.shape[::-1], F32),
+                pltpu.VMEM((1, H), F32),
                 pltpu.VMEM(pair.shape, F32),
                 pltpu.VMEM(pair.shape, BF16),
                 pltpu.VMEM(pair.shape, BF16),
@@ -529,24 +552,15 @@
                 pltpu.VMEM((queries, HP, keys), F32),
                 pltpu.VMEM((queries, HP, keys), F32),
                 pltpu.VMEM((queries, HP, CZ), F32),
-                pltpu.VMEM((sizes[1], HP, LANES), F32),
+                pltpu.VMEM((INNER, HP, LANES), F32),
+                pltpu.VMEM((sizes[1] // INNER, HP, LANES), F32),
                 pltpu.VMEM((queries, 4, LANES), F32),
                 pltpu.VMEM((sizes[1], rows, 4, LANES), F32),
                 pltpu.VMEM((queries, CS // LANES, LANES), F32),
                 pltpu.VMEM((sizes[1], rows, CS // LANES, LANES), F32),
-                dma((4,)),
-                dma((sizes[1],)),
-                dma((sizes[1],)),
-                dma((sizes[0],)),
-                dma((owners,)),
-                dma((sizes[0],)),
-                dma((owners,)),
-                dma((sizes[1],)),
-                dma((sizes[1],)),
-                dma((sizes[1],)),
-                dma((sizes[1],)),
-                dma((sizes[1],)),
-                dma((sizes[1],)),
+                dma((8,)),
+                dma((8,)),
+                dma((8,)),
             ],
             compiler_params=pltpu.CompilerParams(
                 collective_id=0, has_side_effects=True, vmem_limit_bytes=60 * 2**20

time: 52.6 us -> 44.7 us (0.85)
  Pallas kernels: 51.1 us -> 43.2 us
    pallas_call x1, Pallas kernels: 51.1 us -> 43.2 us  [body(): pl.pallas_call(functools.partial(kernel, sizes), out_shape=jax.ShapeDtype...]
where the time goes in v2:
time: 44.7 us; the launch traced here: 44.5 us
  Pallas kernels  43.2 us (97%)
  local copies, waits for them, and re-layouts  1.29 us (3%)
    pallas_call x1, Pallas kernels, body(): pl.pallas_call(functools.partial(kernel, sizes), out_shape=jax.ShapeDtype...  43.2 us
    unnamed x1, local copies, waits for them, and re-layouts  1.29 us

profile of v2, /device:TPU:56, one launch (start us, length us, event | category | flops | bytes accessed | tf_op | source)
XLA Modules:
  0.0 44.5 jit_solution(17857324830463125784)
XLA Ops:
  0.0 43.2 %shard_map.82 = f32[3,384]{1,0:T(4,128)} custom-call(bf16[3,384]{1,0:T(4,128)(2,1)} %singles_hbm.1, f32[3,12]{1,0:T(4,128)} %frames_hbm.1, f32[12,128]{1,0:T(8,128)} %bitcast.6, f32[1,12]{1,0:T(1,128)} %bitcast.7, f32[96,48,128]{2,1,0:T(8,128)} %pair_hbm.1, bf16[336,384]{1,0:T(8,128)(2,1)} %bitcast.5, bf16[816,384]{1,0:T(8,128)(2,1)} %bitcast.4, ...), custom_call_target="tpu_custom_call" | custom-call | tf_op jit(solution)/shard_map/pallas_call | solution.py:531
  43.2 1.3 %copy.10 = f32[3,384]{1,0:T(4,128)} copy(f32[3,384]{1,0:T(4,128)} %shard_map.82) | data formatting | bytes 9216

commit v3 on v2

--- a/solution.py
+++ b/solution.py
@@ -22,6 +22,7 @@
 SPLIT = H * (CH + 4 * PV)
 GROUP = 32
 INNER = 4
+EARLY = 5
 FEAT = H * GROUP
 SCALE = math.sqrt(1.0 / 3.0)
 MESH = pl.DeviceIdType.MESH
@@ -102,12 +103,15 @@
     lse_inner,
     lse_outer,
     point_own,
-    point_all,
+    point_inner,
+    point_mid,
+    point_outer,
     part_own,
     part_all,
     load_sem,
     send_sem,
     recv_sem,
+    ready_sem,
 ):
     row_devs, col_devs = sizes
     rows = singles_ref.shape[0]
@@ -131,26 +135,44 @@
         index = col * owners + slot
         return (index // col_devs, lax.rem(index, col_devs))
 
+    level = outer
+    key_level = key_col // inner_devs
+    source_level = lax.rem(col * owners, col_devs) // inner_devs
+    lower_sources = jnp.clip((level - source_level) * inner_devs, 0, owners)
     barrier = pltpu.get_barrier_semaphore()
+
+    def each(first, last, act):
+        def body(n, carry):
+            act(n)
+            return carry
+
+        lax.fori_loop(first, last, body, 0)
 
     def greet(peer):
         pl.semaphore_signal(barrier, inc=1, device_id=peer, device_id_type=MESH)
 
-    def greet_source(step, carry):
-        slot = lax.rem(key_slot + step, owners)
-
+    def tell(peer):
+        pl.semaphore_signal(
+            ready_sem.at[level], inc=1, device_id=peer, device_id_type=MESH
+        )
+
+    def greet_row(peer):
+        @pl.when(peer != col)
+        def _():
+            greet((row, peer))
+
+    def greet_source(slot):
         @pl.when(jnp.logical_not(jnp.logical_and(own_keys, slot == key_slot)))
         def _():
             greet(source_of(slot))
 
-        return carry
-
-    def greet_row(step, carry):
-        greet((row, lax.rem(col + step, col_devs)))
-        return carry
-
-    lax.fori_loop(0, owners, greet_source, 0)
-    lax.fori_loop(1, col_devs, greet_row, 0)
+    each(level * inner_devs, col_devs, greet_row)
+    each(lower_sources, owners, greet_source)
+
+    @pl.when(key_level > level)
+    def _():
+        each(0, row_devs, lambda peer_row: greet((peer_row, key_col)))
+
     greet(partner)
 
     moves = [
@@ -168,6 +190,11 @@
     ]
     for load in loads:
         load.start()
+
+    near_keys = jnp.where(key_level <= level, row_devs - own_keys.astype(jnp.int32), 0)
+    pl.semaphore_wait(barrier, (level + 1) * inner_devs + near_keys + lower_sources)
+    each(0, level * inner_devs, lambda peer: tell((row, peer)))
+    each(0, lower_sources, lambda slot: tell(source_of(slot)))
 
     loads[0].wait()
     single = singles_ref[...]
@@ -264,8 +291,6 @@
         for t in range(4):
             v_all[key_rows, t, :] = v_feat[:, t * LANES : (t + 1) * LANES]
 
-    pl.semaphore_wait(barrier, owners + col_devs - own_keys.astype(jnp.int32))
-
     def remote(src, dst, peer, kind):
         return pltpu.make_async_remote_copy(
             src_ref=src,
@@ -291,7 +316,7 @@
         def _():
             act(ref.at[pl.ds(0, count * rows)], kind)
 
-    K, Q, V, RELAY, LSE_INNER, LSE_OUTER, POINT, PART = range(8)
+    K, Q, V, RELAY, LSE_INNER, LSE_OUTER, POINT_INNER, POINT_OUTER, PART = range(9)
 
     def each_key_peer(first, step, act):
         def body(n, carry):
@@ -314,10 +339,20 @@
 
     key_rows = pl.ds(key_slot * rows, rows)
     peers = col_devs - 1
-    each_key_peer(0, 1, lambda peer: remote(k_own, k_all.at[key_rows], peer, K).start())
-    each_row_peer(
-        lambda peer: remote(q_all.at[own_rows], q_all.at[own_rows], (row, peer), Q).start()
-    )
+
+    def send_keys():
+        each_key_peer(
+            0, 1, lambda peer: remote(k_own, k_all.at[key_rows], peer, K).start()
+        )
+
+    def send_query(peer):
+        @pl.when(peer != col)
+        def _():
+            mine = q_all.at[own_rows]
+            remote(mine, mine, (row, peer), Q).start()
+
+    pl.when(key_level <= level)(send_keys)
+    each(0, (level + 1) * inner_devs, send_query)
 
     loads[5].wait()
     bias_rows = jnp.concatenate([w_bias_ref[...] * SCALE, jnp.zeros((HP - H, CZ), F32)], 0)
@@ -336,10 +371,20 @@
             small = first[2 * HP :] + second[HP:] + third
             bias_ref[i] = first[0:HP] + (first[HP : 2 * HP] + second[0:HP] + small)
 
+    def next_level(above):
+        far_keys = key_level == above
+        pl.semaphore_wait(
+            ready_sem.at[above], inner_devs + jnp.where(far_keys, row_devs, 0)
+        )
+        pl.when(far_keys)(send_keys)
+        each(above * inner_devs, (above + 1) * inner_devs, send_query)
+
     blocks = queries // 8
-    pl.loop(0, blocks // 2)(bias_block)
+    early = jnp.where(level < EARLY, blocks, 0)
+    pl.loop(0, early)(bias_block)
+    each(level + 1, outer_devs, next_level)
+    pl.loop(early, blocks)(bias_block)
     each_key_peer(0, 2, lambda peer: remote(v_own, v_all.at[key_rows], peer, V).start())
-    pl.loop(blocks // 2, blocks)(bias_block)
 
     of_others(received, k_all, owners, K)
     received(q_all.at[pl.ds(0, peers * rows)], Q)
@@ -371,6 +416,22 @@
         slot = lse_inner.at[inner]
         remote(slot, slot, (row, peer), LSE_INNER).start()
 
+    @pl.loop(0, queries // 8)
+    def _(block):
+        for u in range(8):
+            i = block * 8 + u
+            stacked = jnp.concatenate(pieces(attn_ref[i], 2), 0).astype(BF16)
+            high = dot(stacked, pair_hi[i], NN)
+            low = dot(stacked[0:HP], pair_lo[i], NN)
+            pooled_ref[i] = high[0:HP] + (high[HP:] + low)
+
+    received(lse_inner.at[pl.ds(0, inner_devs - 1)], LSE_INNER)
+    lse_outer[outer] = merged(lse_inner[...])
+    for step in range(1, outer_devs):
+        peer = lax.rem(outer + step, outer_devs) * inner_devs + inner
+        slot = lse_outer.at[outer]
+        remote(slot, slot, (row, peer), LSE_OUTER).start()
+
     direct = lax.rem(col // 2, 2) == core
 
     @pl.when(direct)
@@ -398,30 +459,21 @@
         if t == 3:
             tile = jnp.where(lane128 >= lse_lane, lse, tile)
         point_own[:, t, :] = tile
-    for i in range(rows):
-        point_all[col, i] = point_own[col * rows + i]
-
-    received(lse_inner.at[pl.ds(0, inner_devs - 1)], LSE_INNER)
-    lse_outer[outer] = merged(lse_inner[...])
-    for step in range(1, outer_devs):
-        peer = lax.rem(outer + step, outer_devs) * inner_devs + inner
-        slot = lse_outer.at[outer]
-        remote(slot, slot, (row, peer), LSE_OUTER).start()
-
-    def send_points(peer):
-        theirs = point_own.at[pl.ds(peer * rows, rows)]
-        remote(theirs, point_all.at[col], (row, peer), POINT).start()
-
-    each_row_peer(send_points)
-
-    @pl.loop(0, queries // 8)
-    def _(block):
-        for u in range(8):
-            i = block * 8 + u
-            stacked = jnp.concatenate(pieces(attn_ref[i], 2), 0).astype(BF16)
-            high = dot(stacked, pair_hi[i], NN)
-            low = dot(stacked[0:HP], pair_lo[i], NN)
-            pooled_ref[i] = high[0:HP] + (high[HP:] + low)
+    for z in range(outer_devs):
+        for i in range(rows):
+            point_inner[inner, z * rows + i] = point_own[
+                (z * inner_devs + inner) * rows + i
+            ]
+    for step in range(1, inner_devs):
+        theirs = lax.rem(inner + step, inner_devs)
+        for z in range(outer_devs):
+            sent_rows = pl.ds((z * inner_devs + theirs) * rows, rows)
+            remote(
+                point_own.at[sent_rows],
+                point_inner.at[inner, pl.ds(z * rows, rows)],
+                (row, outer * inner_devs + theirs),
+                POINT_INNER,
+            ).start()
 
     loads[7].wait()
     received(lse_outer.at[pl.ds(0, outer_devs - 1)], LSE_OUTER)
@@ -446,29 +498,59 @@
 
     each_row_peer(send_part)
 
-    received(point_all.at[pl.ds(0, peers)], POINT)
-    shares = []
-    for i in range(rows):
-        sums = point_all[:, i, 3, :]
-        share = jnp.exp(sums - jnp.max(sums, axis=0, keepdims=True))
-        share = share / jnp.sum(share, axis=0, keepdims=True)
-        shares.append(share)
-    shares = jnp.concatenate(pieces(jnp.concatenate(shares, 0), 2), 0).astype(BF16)
     spread = iota((LANES, 4 * LANES), 0) - lse_lane == value_head(
         iota((LANES, 4 * LANES), 1)
     )
     spread = jnp.logical_and(spread, iota((LANES, 4 * LANES), 0) >= lse_lane)
-    wide = dot(shares, jnp.where(spread, 1.0, 0.0).astype(BF16), NN)
-    count = rows * col_devs
-    wide = wide[0:count] + wide[count:]
+    spread = jnp.where(spread, 1.0, 0.0).astype(BF16)
+
+    def spread_heads(shares):
+        wide = dot(jnp.concatenate(pieces(shares, 2), 0).astype(BF16), spread, NN)
+        return wide[0 : shares.shape[0]] + wide[shares.shape[0] :]
+
+    received(point_inner.at[pl.ds(0, inner_devs - 1)], POINT_INNER)
+    count = outer_devs * rows
+    sums = [point_inner[d, :, 3, :] for d in range(inner_devs)]
+    top = functools.reduce(jnp.maximum, sums)
+    shares = [jnp.exp(value - top) for value in sums]
+    total = sum(shares)
+    wide = spread_heads(jnp.concatenate([share / total for share in shares], 0))
+    for t in range(4):
+        tile = sum(
+            point_inner[d, :, t, :]
+            * wide[d * count : (d + 1) * count, t * LANES : (t + 1) * LANES]
+            for d in range(inner_devs)
+        )
+        if t == 3:
+            tile = jnp.where(lane128 >= lse_lane, top + jnp.log(total), tile)
+        point_mid[:, t, :] = tile
+    for i in range(rows):
+        point_outer[outer, i] = point_mid[outer * rows + i]
+    for step in range(1, outer_devs):
+        theirs = lax.rem(outer + step, outer_devs)
+        remote(
+            point_mid.at[pl.ds(theirs * rows, rows)],
+            point_outer.at[outer],
+            (row, theirs * inner_devs + inner),
+            POINT_OUTER,
+        ).start()
+
+    received(point_outer.at[pl.ds(0, outer_devs - 1)], POINT_OUTER)
+    shares = []
+    for i in range(rows):
+        sums = point_outer[:, i, 3, :]
+        share = jnp.exp(sums - jnp.max(sums, axis=0, keepdims=True))
+        shares.append(share / jnp.sum(share, axis=0, keepdims=True))
+    wide = spread_heads(jnp.concatenate(shares, 0))
     kept = jnp.concatenate(
         [
             jnp.concatenate(
                 [
                     jnp.sum(
-                        point_all[:, i, t, :]
+                        point_outer[:, i, t, :]
                         * wide[
-                            i * col_devs : (i + 1) * col_devs, t * LANES : (t + 1) * LANES
+                            i * outer_devs : (i + 1) * outer_devs,
+                            t * LANES : (t + 1) * LANES,
                         ],
                         axis=0,
                         keepdims=True,
@@ -514,7 +596,8 @@
     sent(q_all.at[pl.ds(0, peers * rows)], Q)
     sent(lse_inner.at[pl.ds(0, inner_devs - 1)], LSE_INNER)
     sent(lse_outer.at[pl.ds(0, outer_devs - 1)], LSE_OUTER)
-    sent(point_own.at[pl.ds(0, peers * rows)], POINT)
+    sent(point_inner.at[pl.ds(0, inner_devs - 1)], POINT_INNER)
+    sent(point_outer.at[pl.ds(0, outer_devs - 1)], POINT_OUTER)
     sent(part_own.at[pl.ds(0, peers * rows)], PART)
 
 
@@ -555,12 +638,15 @@
                 pltpu.VMEM((INNER, HP, LANES), F32),
                 pltpu.VMEM((sizes[1] // INNER, HP, LANES), F32),
                 pltpu.VMEM((queries, 4, LANES), F32),
-                pltpu.VMEM((sizes[1], rows, 4, LANES), F32),
+                pltpu.VMEM((INNER, sizes[1] // INNER * rows, 4, LANES), F32),
+                pltpu.VMEM((sizes[1] // INNER * rows, 4, LANES), F32),
+                pltpu.VMEM((sizes[1] // INNER, rows, 4, LANES), F32),
                 pltpu.VMEM((queries, CS // LANES, LANES), F32),
                 pltpu.VMEM((sizes[1], rows, CS // LANES, LANES), F32),
                 dma((8,)),
-                dma((8,)),
-                dma((8,)),
+                dma((9,)),
+                dma((9,)),
+                pltpu.SemaphoreType.REGULAR((sizes[1] // INNER,)),
             ],
             compiler_params=pltpu.CompilerParams(
                 collective_id=0, has_side_effects=True, vmem_limit_bytes=60 * 2**20

time: 44.7 us -> 50.2 us (1.12)
  the two profiles are of different devices: /device:TPU:56 before, /device:TPU:1 now
where the time goes in v3:
time: 50.2 us; the launch traced here: 50.1 us
  Pallas kernels  48.8 us (97%)
  local copies, waits for them, and re-layouts  1.29 us (3%)
    pallas_call x1, Pallas kernels, body(): pl.pallas_call(functools.partial(kernel, sizes), out_shape=jax.ShapeDtype...  48.8 us
    unnamed x1, local copies, waits for them, and re-layouts  1.29 us

profile of v3, /device:TPU:1, one launch (start us, length us, event | category | flops | bytes accessed | tf_op | source)
XLA Modules:
  0.0 50.1 jit_solution(10607476892688549607)
XLA Ops:
  0.0 48.8 %shard_map.82 = f32[3,384]{1,0:T(4,128)} custom-call(bf16[3,384]{1,0:T(4,128)(2,1)} %singles_hbm.1, f32[3,12]{1,0:T(4,128)} %frames_hbm.1, f32[12,128]{1,0:T(8,128)} %bitcast.6, f32[1,12]{1,0:T(1,128)} %bitcast.7, f32[96,48,128]{2,1,0:T(8,128)} %pair_hbm.1, bf16[336,384]{1,0:T(8,128)(2,1)} %bitcast.5, bf16[816,384]{1,0:T(8,128)(2,1)} %bitcast.4, ...), custom_call_target="tpu_custom_call" | custom-call | tf_op jit(solution)/shard_map/pallas_call | solution.py:614
  48.8 1.3 %copy.10 = f32[3,384]{1,0:T(4,128)} copy(f32[3,384]{1,0:T(4,128)} %shard_map.82) | data formatting | bytes 9216

commit v4 on v2

--- a/solution.py
+++ b/solution.py
@@ -92,8 +92,8 @@
     w_keyval_ref,
     w_out_ref,
     q_all,
-    k_own,
-    v_own,
+    k_chunk,
+    v_chunk,
     k_all,
     v_all,
     bias_ref,
@@ -102,7 +102,9 @@
     lse_inner,
     lse_outer,
     point_own,
-    point_all,
+    point_inner,
+    point_mid,
+    point_outer,
     part_own,
     part_all,
     load_sem,
@@ -116,41 +118,42 @@
     row = lax.axis_index("row")
     col = lax.axis_index("col")
 
-    me = row * col_devs + col
-    key_col = me // owners
-    key_slot = lax.rem(me, owners)
-    own_keys = key_col == col
     core = lax.rem(row, 2)
+    y = row // 2
+    y_devs = row_devs // 2
     partner = (row + 1 - 2 * core, col)
     inner_devs = INNER
     outer_devs = col_devs // INNER
     inner = lax.rem(col, INNER)
     outer = col // INNER
-
-    def source_of(slot):
-        index = col * owners + slot
-        return (index // col_devs, lax.rem(index, col_devs))
+    key_slot = lax.rem(col, owners)
+
+    def key_col_of(source_y):
+        return ((2 * source_y + core) * col_devs + col) // owners
+
+    direct = lax.rem(col * owners // col_devs, 2) == core
+    own_source_y = (col * owners) // (2 * col_devs)
+    own_keys = key_col_of(own_source_y) == col
 
     barrier = pltpu.get_barrier_semaphore()
 
     def greet(peer):
         pl.semaphore_signal(barrier, inc=1, device_id=peer, device_id_type=MESH)
 
-    def greet_source(step, carry):
-        slot = lax.rem(key_slot + step, owners)
-
-        @pl.when(jnp.logical_not(jnp.logical_and(own_keys, slot == key_slot)))
-        def _():
-            greet(source_of(slot))
-
-        return carry
-
-    def greet_row(step, carry):
-        greet((row, lax.rem(col + step, col_devs)))
-        return carry
-
-    lax.fori_loop(0, owners, greet_source, 0)
-    lax.fori_loop(1, col_devs, greet_row, 0)
+    def row_peers():
+        half = col_devs // 2
+        steps = sorted(range(1, col_devs), key=lambda step: abs(step - half))
+        return [lax.rem(col + step, col_devs) for step in steps]
+
+    def y_peers():
+        half = y_devs // 2
+        steps = sorted(range(1, y_devs), key=lambda step: abs(step - half))
+        return [(2 * lax.rem(y + step, y_devs) + core, col) for step in steps]
+
+    for peer in row_peers():
+        greet((row, peer))
+    for peer in y_peers():
+        greet(peer)
     greet(partner)
 
     moves = [
@@ -253,18 +256,11 @@
     for t in range(FEAT // LANES):
         part = slice(t * LANES, (t + 1) * LANES)
         q_all[own_rows, t, :] = q_feat[0:rows, part]
-        k_own[:, t, :] = k_feat[rows : 2 * rows, part]
+        k_chunk[y, :, t, :] = k_feat[rows : 2 * rows, part]
     for t in range(4):
-        v_own[:, t, :] = v_feat[:, t * LANES : (t + 1) * LANES]
-
-    @pl.when(own_keys)
-    def _():
-        for t in range(FEAT // LANES):
-            k_all[key_rows, t, :] = k_feat[rows : 2 * rows, t * LANES : (t + 1) * LANES]
-        for t in range(4):
-            v_all[key_rows, t, :] = v_feat[:, t * LANES : (t + 1) * LANES]
-
-    pl.semaphore_wait(barrier, owners + col_devs - own_keys.astype(jnp.int32))
+        v_chunk[y, :, t, :] = v_feat[:, t * LANES : (t + 1) * LANES]
+
+    pl.semaphore_wait(barrier, col_devs + y_devs - 1)
 
     def remote(src, dst, peer, kind):
         return pltpu.make_async_remote_copy(
@@ -282,42 +278,42 @@
     def received(ref, kind):
         remote(ref, ref, partner, kind).wait_recv()
 
-    def of_others(act, ref, count, kind):
+    KY, VY, K, V, Q, KR, VR, LSE_INNER, LSE_OUTER, POINT_INNER, POINT_OUTER, PART = range(12)
+    key_rows = pl.ds(key_slot * rows, rows)
+    peers = col_devs - 1
+    for peer in y_peers():
+        remote(k_chunk.at[y], k_chunk.at[y], peer, KY).start()
+    for peer in row_peers():
+        remote(q_all.at[own_rows], q_all.at[own_rows], (row, peer), Q).start()
+    for peer in y_peers():
+        remote(v_chunk.at[y], v_chunk.at[y], peer, VY).start()
+
+    def forward(chunk, whole, kind):
+        def body(step, carry):
+            source_y = lax.rem(outer + step, y_devs)
+            peer = key_col_of(source_y)
+
+            @pl.when(peer != col)
+            def _():
+                remote(chunk.at[source_y], whole.at[key_rows], (row, peer), kind).start()
+
+            return carry
+
+        lax.fori_loop(0, y_devs, body, 0)
+
         @pl.when(own_keys)
         def _():
-            act(ref.at[pl.ds(0, (count - 1) * rows)], kind)
+            for i in range(rows):
+                whole[key_slot * rows + i] = chunk[own_source_y, i]
+
+    def of_sources(act, whole, count, kind):
+        @pl.when(own_keys)
+        def _():
+            act(whole.at[pl.ds(0, (count - 1) * rows)], kind)
 
         @pl.when(jnp.logical_not(own_keys))
         def _():
-            act(ref.at[pl.ds(0, count * rows)], kind)
-
-    K, Q, V, RELAY, LSE_INNER, LSE_OUTER, POINT, PART = range(8)
-
-    def each_key_peer(first, step, act):
-        def body(n, carry):
-            peer_row = lax.rem(row + n * step + first, row_devs)
-
-            @pl.when(jnp.logical_not(jnp.logical_and(own_keys, peer_row == row)))
-            def _():
-                act((peer_row, key_col))
-
-            return carry
-
-        lax.fori_loop(0, row_devs // step, body, 0)
-
-    def each_row_peer(act):
-        def body(step, carry):
-            act(lax.rem(col + step, col_devs))
-            return carry
-
-        lax.fori_loop(1, col_devs, body, 0)
-
-    key_rows = pl.ds(key_slot * rows, rows)
-    peers = col_devs - 1
-    each_key_peer(0, 1, lambda peer: remote(k_own, k_all.at[key_rows], peer, K).start())
-    each_row_peer(
-        lambda peer: remote(q_all.at[own_rows], q_all.at[own_rows], (row, peer), Q).start()
-    )
+            act(whole.at[pl.ds(0, count * rows)], kind)
 
     loads[5].wait()
     bias_rows = jnp.concatenate([w_bias_ref[...] * SCALE, jnp.zeros((HP - H, CZ), F32)], 0)
@@ -338,11 +334,27 @@
 
     blocks = queries // 8
     pl.loop(0, blocks // 2)(bias_block)
-    each_key_peer(0, 2, lambda peer: remote(v_own, v_all.at[key_rows], peer, V).start())
+    received(k_chunk.at[pl.ds(0, y_devs - 1)], KY)
+    forward(k_chunk, k_all, K)
+    received(v_chunk.at[pl.ds(0, y_devs - 1)], VY)
+    forward(v_chunk, v_all, V)
     pl.loop(blocks // 2, blocks)(bias_block)
 
-    of_others(received, k_all, owners, K)
+    @pl.when(direct)
+    def _():
+        of_sources(received, k_all, owners, K)
+        remote(k_all, k_all, partner, KR).start()
+
     received(q_all.at[pl.ds(0, peers * rows)], Q)
+
+    @pl.when(direct)
+    def _():
+        of_sources(received, v_all, owners, V)
+        remote(v_all, v_all, partner, VR).start()
+
+    @pl.when(jnp.logical_not(direct))
+    def _():
+        received(k_all, KR)
 
     lse_lane = VALUE % LANES
     lane128 = iota((1, LANES), 1)
@@ -371,16 +383,9 @@
         slot = lse_inner.at[inner]
         remote(slot, slot, (row, peer), LSE_INNER).start()
 
-    direct = lax.rem(col // 2, 2) == core
-
-    @pl.when(direct)
-    def _():
-        of_others(received, v_all, owners, V)
-        remote(v_all, v_all, partner, RELAY).start()
-
     @pl.when(jnp.logical_not(direct))
     def _():
-        received(v_all, RELAY)
+        received(v_all, VR)
 
     values = jnp.concatenate([v_all[:, t, :] for t in range(4)], 1)
     v1, v2 = [piece.astype(BF16) for piece in pieces(values, 2)]
@@ -398,8 +403,21 @@
         if t == 3:
             tile = jnp.where(lane128 >= lse_lane, lse, tile)
         point_own[:, t, :] = tile
-    for i in range(rows):
-        point_all[col, i] = point_own[col * rows + i]
+    for z in range(outer_devs):
+        for i in range(rows):
+            point_inner[inner, z * rows + i] = point_own[
+                (z * inner_devs + inner) * rows + i
+            ]
+    for step in range(1, inner_devs):
+        theirs = lax.rem(inner + step, inner_devs)
+        for z in range(outer_devs):
+            sent_rows = pl.ds((z * inner_devs + theirs) * rows, rows)
+            remote(
+                point_own.at[sent_rows],
+                point_inner.at[inner, pl.ds(z * rows, rows)],
+                (row, outer * inner_devs + theirs),
+                POINT_INNER,
+            ).start()
 
     received(lse_inner.at[pl.ds(0, inner_devs - 1)], LSE_INNER)
     lse_outer[outer] = merged(lse_inner[...])
@@ -407,12 +425,6 @@
         peer = lax.rem(outer + step, outer_devs) * inner_devs + inner
         slot = lse_outer.at[outer]
         remote(slot, slot, (row, peer), LSE_OUTER).start()
-
-    def send_points(peer):
-        theirs = point_own.at[pl.ds(peer * rows, rows)]
-        remote(theirs, point_all.at[col], (row, peer), POINT).start()
-
-    each_row_peer(send_points)
 
     @pl.loop(0, queries // 8)
     def _(block):
@@ -422,6 +434,43 @@
             high = dot(stacked, pair_hi[i], NN)
             low = dot(stacked[0:HP], pair_lo[i], NN)
             pooled_ref[i] = high[0:HP] + (high[HP:] + low)
+
+    spread = iota((LANES, 4 * LANES), 0) - lse_lane == value_head(
+        iota((LANES, 4 * LANES), 1)
+    )
+    spread = jnp.logical_and(spread, iota((LANES, 4 * LANES), 0) >= lse_lane)
+    spread = jnp.where(spread, 1.0, 0.0).astype(BF16)
+
+    def spread_heads(shares):
+        wide = dot(jnp.concatenate(pieces(shares, 2), 0).astype(BF16), spread, NN)
+        return wide[0 : shares.shape[0]] + wide[shares.shape[0] :]
+
+    received(point_inner.at[pl.ds(0, inner_devs - 1)], POINT_INNER)
+    count = outer_devs * rows
+    sums = [point_inner[d, :, 3, :] for d in range(inner_devs)]
+    top = functools.reduce(jnp.maximum, sums)
+    shares = [jnp.exp(value - top) for value in sums]
+    total = sum(shares)
+    wide = spread_heads(jnp.concatenate([share / total for share in shares], 0))
+    for t in range(4):
+        tile = sum(
+            point_inner[d, :, t, :]
+            * wide[d * count : (d + 1) * count, t * LANES : (t + 1) * LANES]
+            for d in range(inner_devs)
+        )
+        if t == 3:
+            tile = jnp.where(lane128 >= lse_lane, top + jnp.log(total), tile)
+        point_mid[:, t, :] = tile
+    for i in range(rows):
+        point_outer[outer, i] = point_mid[outer * rows + i]
+    for step in range(1, outer_devs):
+        theirs = lax.rem(outer + step, outer_devs)
+        remote(
+            point_mid.at[pl.ds(theirs * rows, rows)],
+            point_outer.at[outer],
+            (row, theirs * inner_devs + inner),
+            POINT_OUTER,
+        ).start()
 
     loads[7].wait()
     received(lse_outer.at[pl.ds(0, outer_devs - 1)], LSE_OUTER)
@@ -439,36 +488,26 @@
         part_own[:, t, :] = projected[:, t * LANES : (t + 1) * LANES]
     for i in range(rows):
         part_all[col, i] = part_own[col * rows + i]
-
-    def send_part(peer):
+    for peer in row_peers():
         theirs = part_own.at[pl.ds(peer * rows, rows)]
         remote(theirs, part_all.at[col], (row, peer), PART).start()
 
-    each_row_peer(send_part)
-
-    received(point_all.at[pl.ds(0, peers)], POINT)
+    received(point_outer.at[pl.ds(0, outer_devs - 1)], POINT_OUTER)
     shares = []
     for i in range(rows):
-        sums = point_all[:, i, 3, :]
+        sums = point_outer[:, i, 3, :]
         share = jnp.exp(sums - jnp.max(sums, axis=0, keepdims=True))
-        share = share / jnp.sum(share, axis=0, keepdims=True)
-        shares.append(share)
-    shares = jnp.concatenate(pieces(jnp.concatenate(shares, 0), 2), 0).astype(BF16)
-    spread = iota((LANES, 4 * LANES), 0) - lse_lane == value_head(
-        iota((LANES, 4 * LANES), 1)
-    )
-    spread = jnp.logical_and(spread, iota((LANES, 4 * LANES), 0) >= lse_lane)
-    wide = dot(shares, jnp.where(spread, 1.0, 0.0).astype(BF16), NN)
-    count = rows * col_devs
-    wide = wide[0:count] + wide[count:]
+        shares.append(share / jnp.sum(share, axis=0, keepdims=True))
+    wide = spread_heads(jnp.concatenate(shares, 0))
     kept = jnp.concatenate(
         [
             jnp.concatenate(
                 [
                     jnp.sum(
-                        point_all[:, i, t, :]
+                        point_outer[:, i, t, :]
                         * wide[
-                            i * col_devs : (i + 1) * col_devs, t * LANES : (t + 1) * LANES
+                            i * outer_devs : (i + 1) * outer_devs,
+                            t * LANES : (t + 1) * LANES,
                         ],
                         axis=0,
                         keepdims=True,
@@ -504,17 +543,21 @@
         ]
         out_ref[:, part] = update[:, part] + jnp.concatenate(terms, 0)
 
-    of_others(sent, k_all, row_devs, K)
-    of_others(sent, v_all, row_devs // 2, V)
+    sent(k_chunk.at[pl.ds(0, y_devs - 1)], KY)
+    sent(v_chunk.at[pl.ds(0, y_devs - 1)], VY)
+    of_sources(sent, k_all, y_devs, K)
+    of_sources(sent, v_all, y_devs, V)
 
     @pl.when(direct)
     def _():
-        sent(v_all, RELAY)
+        sent(k_all, KR)
+        sent(v_all, VR)
 
     sent(q_all.at[pl.ds(0, peers * rows)], Q)
     sent(lse_inner.at[pl.ds(0, inner_devs - 1)], LSE_INNER)
     sent(lse_outer.at[pl.ds(0, outer_devs - 1)], LSE_OUTER)
-    sent(point_own.at[pl.ds(0, peers * rows)], POINT)
+    sent(point_inner.at[pl.ds(0, inner_devs - 1)], POINT_INNER)
+    sent(point_outer.at[pl.ds(0, outer_devs - 1)], POINT_OUTER)
     sent(part_own.at[pl.ds(0, peers * rows)], PART)
 
 
@@ -524,7 +567,6 @@
     def body(singles, pair, frames, w_query, w_keyval, w_bias, head_weights, w_out):
         rows = singles.shape[0]
         queries, keys = pair.shape[0], pair.shape[1]
-        owners = keys // rows
         vmem = pl.BlockSpec(memory_space=pltpu.VMEM)
         hbm = pl.BlockSpec(memory_space=pl.ANY)
         dma = pltpu.SemaphoreType.DMA
@@ -545,8 +587,8 @@
                 pltpu.VMEM(w_keyval.shape[::-1], w_keyval.dtype),
                 pltpu.VMEM(w_out.shape, w_out.dtype),
                 pltpu.VMEM((queries, FEAT // LANES, LANES), F32),
-                pltpu.VMEM((rows, FEAT // LANES, LANES), F32),
-                pltpu.VMEM((rows, 4, LANES), F32),
+                pltpu.VMEM((sizes[0] // 2, rows, FEAT // LANES, LANES), F32),
+                pltpu.VMEM((sizes[0] // 2, rows, 4, LANES), F32),
                 pltpu.VMEM((keys, FEAT // LANES, LANES), F32),
                 pltpu.VMEM((keys, 4, LANES), F32),
                 pltpu.VMEM((queries, HP, keys), F32),
@@ -555,12 +597,14 @@
                 pltpu.VMEM((INNER, HP, LANES), F32),
                 pltpu.VMEM((sizes[1] // INNER, HP, LANES), F32),
                 pltpu.VMEM((queries, 4, LANES), F32),
-                pltpu.VMEM((sizes[1], rows, 4, LANES), F32),
+                pltpu.VMEM((INNER, sizes[1] // INNER * rows, 4, LANES), F32),
+                pltpu.VMEM((sizes[1] // INNER * rows, 4, LANES), F32),
+                pltpu.VMEM((sizes[1] // INNER, rows, 4, LANES), F32),
                 pltpu.VMEM((queries, CS // LANES, LANES), F32),
                 pltpu.VMEM((sizes[1], rows, CS // LANES, LANES), F32),
                 dma((8,)),
-                dma((8,)),
-                dma((8,)),
+                dma((12,)),
+                dma((12,)),
             ],
             compiler_params=pltpu.CompilerParams(
                 collective_id=0, has_side_effects=True, vmem_limit_bytes=60 * 2**20

time: 44.7 us -> 48 us (1.074)
  the two profiles are of different devices: /device:TPU:56 before, /device:TPU:1 now
where the time goes in v4:
time: 48 us; the launch traced here: 47.8 us
  Pallas kernels  46.5 us (97%)
  local copies, waits for them, and re-layouts  1.29 us (3%)
    pallas_call x1, Pallas kernels, body(): pl.pallas_call(functools.partial(kernel, sizes), out_shape=jax.ShapeDtype...  46.5 us
    unnamed x1, local copies, waits for them, and re-layouts  1.29 us

profile of v4, /device:TPU:1, one launch (start us, length us, event | category | flops | bytes accessed | tf_op | source)
XLA Modules:
  0.0 47.8 jit_solution(4142755701779848453)
XLA Ops:
  0.0 46.5 %shard_map.82 = f32[3,384]{1,0:T(4,128)} custom-call(bf16[3,384]{1,0:T(4,128)(2,1)} %singles_hbm.1, f32[3,12]{1,0:T(4,128)} %frames_hbm.1, f32[12,128]{1,0:T(8,128)} %bitcast.6, f32[1,12]{1,0:T(1,128)} %bitcast.7, f32[96,48,128]{2,1,0:T(8,128)} %pair_hbm.1, bf16[336,384]{1,0:T(8,128)(2,1)} %bitcast.5, bf16[816,384]{1,0:T(8,128)(2,1)} %bitcast.4, ...), custom_call_target="tpu_custom_call" | custom-call | tf_op jit(solution)/shard_map/pallas_call | solution.py:573
  46.5 1.3 %copy.10 = f32[3,384]{1,0:T(4,128)} copy(f32[3,384]{1,0:T(4,128)} %shard_map.82) | data formatting | bytes 9216

commit v5 on v2

--- a/solution.py
+++ b/solution.py
@@ -21,7 +21,6 @@
 VALUE = SCALAR + 3 * H * PV
 SPLIT = H * (CH + 4 * PV)
 GROUP = 32
-INNER = 4
 FEAT = H * GROUP
 SCALE = math.sqrt(1.0 / 3.0)
 MESH = pl.DeviceIdType.MESH
@@ -57,11 +56,6 @@
         + frame[:, 9 + a : 10 + a]
         for a in range(3)
     ]
-
-
-def merged(sums):
-    top = jnp.max(sums, axis=0)
-    return top + jnp.log(jnp.sum(jnp.exp(sums - top[None]), axis=0))
 
 
 def value_head(lane):
@@ -98,11 +92,6 @@
     v_all,
     bias_ref,
     attn_ref,
-    pooled_ref,
-    lse_inner,
-    lse_outer,
-    point_own,
-    point_all,
     part_own,
     part_all,
     load_sem,
@@ -120,17 +109,15 @@
     key_col = me // owners
     key_slot = lax.rem(me, owners)
     own_keys = key_col == col
-    core = lax.rem(row, 2)
-    partner = (row + 1 - 2 * core, col)
-    inner_devs = INNER
-    outer_devs = col_devs // INNER
-    inner = lax.rem(col, INNER)
-    outer = col // INNER
 
     def source_of(slot):
         index = col * owners + slot
         return (index // col_devs, lax.rem(index, col_devs))
 
+    def far_first(count):
+        return sorted(range(1, count), key=lambda step: abs(step - count // 2))
+
+    row_peers = [lax.rem(col + step, col_devs) for step in far_first(col_devs)]
     barrier = pltpu.get_barrier_semaphore()
 
     def greet(peer):
@@ -145,13 +132,9 @@
 
         return carry
 
-    def greet_row(step, carry):
-        greet((row, lax.rem(col + step, col_devs)))
-        return carry
-
     lax.fori_loop(0, owners, greet_source, 0)
-    lax.fori_loop(1, col_devs, greet_row, 0)
-    greet(partner)
+    for peer in row_peers:
+        greet((row, peer))
 
     moves = [
         (singles_hbm, singles_ref),
@@ -257,6 +240,8 @@
     for t in range(4):
         v_own[:, t, :] = v_feat[:, t * LANES : (t + 1) * LANES]
 
+    key_rows = pl.ds(key_slot * rows, rows)
+
     @pl.when(own_keys)
     def _():
         for t in range(FEAT // LANES):
@@ -264,7 +249,7 @@
         for t in range(4):
             v_all[key_rows, t, :] = v_feat[:, t * LANES : (t + 1) * LANES]
 
-    pl.semaphore_wait(barrier, owners + col_devs - own_keys.astype(jnp.int32))
+    pl.semaphore_wait(barrier, owners + col_devs - 1 - own_keys.astype(jnp.int32))
 
     def remote(src, dst, peer, kind):
         return pltpu.make_async_remote_copy(
@@ -277,10 +262,25 @@
         )
 
     def sent(ref, kind):
-        remote(ref, ref, partner, kind).wait_send()
+        remote(ref, ref, (row, row_peers[0]), kind).wait_send()
 
     def received(ref, kind):
-        remote(ref, ref, partner, kind).wait_recv()
+        remote(ref, ref, (row, row_peers[0]), kind).wait_recv()
+
+    K, Q, V, PART = range(4)
+    peers = col_devs - 1
+
+    def send_keys(src, dst, kind):
+        def body(step, carry):
+            peer_row = lax.rem(row + row_devs // 2 + step, row_devs)
+
+            @pl.when(jnp.logical_not(jnp.logical_and(own_keys, peer_row == row)))
+            def _():
+                remote(src, dst.at[key_rows], (peer_row, key_col), kind).start()
+
+            return carry
+
+        lax.fori_loop(0, row_devs, body, 0)
 
     def of_others(act, ref, count, kind):
         @pl.when(own_keys)
@@ -291,33 +291,9 @@
         def _():
             act(ref.at[pl.ds(0, count * rows)], kind)
 
-    K, Q, V, RELAY, LSE_INNER, LSE_OUTER, POINT, PART = range(8)
-
-    def each_key_peer(first, step, act):
-        def body(n, carry):
-            peer_row = lax.rem(row + n * step + first, row_devs)
-
-            @pl.when(jnp.logical_not(jnp.logical_and(own_keys, peer_row == row)))
-            def _():
-                act((peer_row, key_col))
-
-            return carry
-
-        lax.fori_loop(0, row_devs // step, body, 0)
-
-    def each_row_peer(act):
-        def body(step, carry):
-            act(lax.rem(col + step, col_devs))
-            return carry
-
-        lax.fori_loop(1, col_devs, body, 0)
-
-    key_rows = pl.ds(key_slot * rows, rows)
-    peers = col_devs - 1
-    each_key_peer(0, 1, lambda peer: remote(k_own, k_all.at[key_rows], peer, K).start())
-    each_row_peer(
-        lambda peer: remote(q_all.at[own_rows], q_all.at[own_rows], (row, peer), Q).start()
-    )
+    send_keys(k_own, k_all, K)
+    for peer in row_peers:
+        remote(q_all.at[own_rows], q_all.at[own_rows], (row, peer), Q).start()
 
     loads[5].wait()
     bias_rows = jnp.concatenate([w_bias_ref[...] * SCALE, jnp.zeros((HP - H, CZ), F32)], 0)
@@ -338,7 +314,7 @@
 
     blocks = queries // 8
     pl.loop(0, blocks // 2)(bias_block)
-    each_key_peer(0, 2, lambda peer: remote(v_own, v_all.at[key_rows], peer, V).start())
+    send_keys(v_own, v_all, V)
     pl.loop(blocks // 2, blocks)(bias_block)
 
     of_others(received, k_all, owners, K)
@@ -363,25 +339,7 @@
             attn_ref[:, h, :] = exponent * (1.0 / total)
             lse = jnp.where(lane128 == lse_lane + h, top + jnp.log(total), lse)
 
-    turned = jnp.concatenate([lse, jnp.zeros((LANES - queries, LANES), F32)], 0).T
-    own_lse = turned[lse_lane : lse_lane + HP]
-    lse_inner[inner] = own_lse
-    for step in range(1, inner_devs):
-        peer = outer * inner_devs + lax.rem(inner + step, inner_devs)
-        slot = lse_inner.at[inner]
-        remote(slot, slot, (row, peer), LSE_INNER).start()
-
-    direct = lax.rem(col // 2, 2) == core
-
-    @pl.when(direct)
-    def _():
-        of_others(received, v_all, owners, V)
-        remote(v_all, v_all, partner, RELAY).start()
-
-    @pl.when(jnp.logical_not(direct))
-    def _():
-        received(v_all, RELAY)
-
+    of_others(received, v_all, owners, V)
     values = jnp.concatenate([v_all[:, t, :] for t in range(4)], 1)
     v1, v2 = [piece.astype(BF16) for piece in pieces(values, 2)]
     lane_of = value_head(iota((1, 4 * LANES), 1))
@@ -397,90 +355,76 @@
         tile = gathered[:, t * LANES : (t + 1) * LANES]
         if t == 3:
             tile = jnp.where(lane128 >= lse_lane, lse, tile)
-        point_own[:, t, :] = tile
-    for i in range(rows):
-        point_all[col, i] = point_own[col * rows + i]
-
-    received(lse_inner.at[pl.ds(0, inner_devs - 1)], LSE_INNER)
-    lse_outer[outer] = merged(lse_inner[...])
-    for step in range(1, outer_devs):
-        peer = lax.rem(outer + step, outer_devs) * inner_devs + inner
-        slot = lse_outer.at[outer]
-        remote(slot, slot, (row, peer), LSE_OUTER).start()
-
-    def send_points(peer):
-        theirs = point_own.at[pl.ds(peer * rows, rows)]
-        remote(theirs, point_all.at[col], (row, peer), POINT).start()
-
-    each_row_peer(send_points)
-
-    @pl.loop(0, queries // 8)
-    def _(block):
-        for u in range(8):
-            i = block * 8 + u
-            stacked = jnp.concatenate(pieces(attn_ref[i], 2), 0).astype(BF16)
-            high = dot(stacked, pair_hi[i], NN)
-            low = dot(stacked[0:HP], pair_lo[i], NN)
-            pooled_ref[i] = high[0:HP] + (high[HP:] + low)
-
-    loads[7].wait()
-    received(lse_outer.at[pl.ds(0, outer_devs - 1)], LSE_OUTER)
-    factor = jnp.exp(own_lse - merged(lse_outer[...]))
-    factor = jnp.concatenate([factor, jnp.zeros((LANES - HP, LANES), F32)], 0).T
-    projected = jnp.zeros((queries, CS), F32)
-    for h in range(0, H, 2):
-        scaled = jnp.concatenate(
-            [pooled_ref[:, g, :] * factor[0:queries, g : g + 1] for g in (h, h + 1)], 1
-        )
-        stacked = jnp.concatenate(pieces(scaled, 2), 0).astype(BF16)
-        share = dot(stacked, w_out_ref[SPLIT + h * CZ : SPLIT + (h + 2) * CZ, :], NN)
-        projected = projected + (share[0:queries] + share[queries:])
-    for t in range(CS // LANES):
-        part_own[:, t, :] = projected[:, t * LANES : (t + 1) * LANES]
+        part_own[:, HP - 4 + t, :] = tile
+
+    def pool(n, carry):
+        half = col_devs // 2
+        steps = [half + 2 * n, half - 1 - 2 * n, half + 2 * n + 1, half - 2 - 2 * n]
+        to = [lax.rem(col + step, col_devs) for step in steps]
+        for owner in to:
+            for i in range(rows):
+                at = owner * rows + i
+                stacked = jnp.concatenate(pieces(attn_ref[at], 2), 0).astype(BF16)
+                high = dot(stacked, pair_hi[at], NN)
+                low = dot(stacked[0:HP], pair_lo[at], NN)
+                part_own[at, 0:H, :] = (high[0:HP] + (high[HP:] + low))[0:H]
+        for owner in to:
+
+            @pl.when(owner != col)
+            def _():
+                theirs = part_own.at[pl.ds(owner * rows, rows)]
+                remote(theirs, part_all.at[col], (row, owner), PART).start()
+
+        return carry
+
+    lax.fori_loop(0, col_devs // 4, pool, 0)
     for i in range(rows):
         part_all[col, i] = part_own[col * rows + i]
 
-    def send_part(peer):
-        theirs = part_own.at[pl.ds(peer * rows, rows)]
-        remote(theirs, part_all.at[col], (row, peer), PART).start()
-
-    each_row_peer(send_part)
-
-    received(point_all.at[pl.ds(0, peers)], POINT)
+    spread = iota((LANES, 4 * LANES), 0) - lse_lane == value_head(
+        iota((LANES, 4 * LANES), 1)
+    )
+    spread = jnp.logical_and(spread, iota((LANES, 4 * LANES), 0) >= lse_lane)
+    spread = jnp.where(spread, 1.0, 0.0).astype(BF16)
+    loads[7].wait()
+    received(part_all.at[pl.ds(0, peers)], PART)
     shares = []
     for i in range(rows):
-        sums = point_all[:, i, 3, :]
+        sums = part_all[:, i, HP - 1, :]
         share = jnp.exp(sums - jnp.max(sums, axis=0, keepdims=True))
-        share = share / jnp.sum(share, axis=0, keepdims=True)
-        shares.append(share)
-    shares = jnp.concatenate(pieces(jnp.concatenate(shares, 0), 2), 0).astype(BF16)
-    spread = iota((LANES, 4 * LANES), 0) - lse_lane == value_head(
-        iota((LANES, 4 * LANES), 1)
-    )
-    spread = jnp.logical_and(spread, iota((LANES, 4 * LANES), 0) >= lse_lane)
-    wide = dot(shares, jnp.where(spread, 1.0, 0.0).astype(BF16), NN)
+        shares.append(share / jnp.sum(share, axis=0, keepdims=True))
     count = rows * col_devs
+    wide = dot(jnp.concatenate(pieces(jnp.concatenate(shares, 0), 2), 0).astype(BF16), spread, NN)
     wide = wide[0:count] + wide[count:]
+
+    def over_devices(tiles):
+        return jnp.concatenate([jnp.sum(tile, axis=0, keepdims=True) for tile in tiles], 0)
+
     kept = jnp.concatenate(
         [
-            jnp.concatenate(
-                [
-                    jnp.sum(
-                        point_all[:, i, t, :]
-                        * wide[
-                            i * col_devs : (i + 1) * col_devs, t * LANES : (t + 1) * LANES
-                        ],
-                        axis=0,
-                        keepdims=True,
-                    )
-                    for t in range(4)
-                ],
-                1,
+            over_devices(
+                part_all[:, i, HP - 4 + t, :]
+                * wide[i * col_devs : (i + 1) * col_devs, t * LANES : (t + 1) * LANES]
+                for i in range(rows)
             )
-            for i in range(rows)
+            for t in range(4)
         ],
-        0,
-    )
+        1,
+    )
+    pooled = jnp.concatenate(
+        [
+            over_devices(
+                part_all[:, i, h, :] * shares[i][:, lse_lane + h : lse_lane + h + 1]
+                for i in range(rows)
+            )
+            for h in range(H)
+        ],
+        1,
+    )
+    pooled = jnp.concatenate([pooled, jnp.zeros((8 - rows, H * CZ), F32)], 0)
+    pooled = jnp.concatenate(pieces(pooled, 2), 0).astype(BF16)
+    projected = dot(pooled, w_out_ref[SPLIT:, :], NN)
+    projected = projected[0:rows] + projected[8 : 8 + rows]
     wide = H * PV
     relative = [
         kept[:, SCALAR + b * wide : SCALAR + (b + 1) * wide] - frame[:, 9 + b : 10 + b]
@@ -494,28 +438,12 @@
     ]
     length = jnp.sqrt(local[0] ** 2 + local[1] ** 2 + local[2] ** 2 + 1.0)
     features = jnp.concatenate([kept[:, :SCALAR]] + local + [length], 1).astype(BF16)
-    update = dot(features, w_out_ref[0:SPLIT, :], NN)
-
-    received(part_all.at[pl.ds(0, peers)], PART)
-    for t in range(CS // LANES):
-        part = slice(t * LANES, (t + 1) * LANES)
-        terms = [
-            jnp.sum(part_all[:, i, t, :], axis=0, keepdims=True) for i in range(rows)
-        ]
-        out_ref[:, part] = update[:, part] + jnp.concatenate(terms, 0)
+    out_ref[...] = dot(features, w_out_ref[0:SPLIT, :], NN) + projected
 
     of_others(sent, k_all, row_devs, K)
-    of_others(sent, v_all, row_devs // 2, V)
-
-    @pl.when(direct)
-    def _():
-        sent(v_all, RELAY)
-
+    of_others(sent, v_all, row_devs, V)
     sent(q_all.at[pl.ds(0, peers * rows)], Q)
-    sent(lse_inner.at[pl.ds(0, inner_devs - 1)], LSE_INNER)
-    sent(lse_outer.at[pl.ds(0, outer_devs - 1)], LSE_OUTER)
-    sent(point_own.at[pl.ds(0, peers * rows)], POINT)
-    sent(part_own.at[pl.ds(0, peers * rows)], PART)
+    sent(part_all.at[pl.ds(0, peers)], PART)
 
 
 def solution(mesh):
@@ -524,7 +452,6 @@
     def body(singles, pair, frames, w_query, w_keyval, w_bias, head_weights, w_out):
         rows = singles.shape[0]
         queries, keys = pair.shape[0], pair.shape[1]
-        owners = keys // rows
         vmem = pl.BlockSpec(memory_space=pltpu.VMEM)
         hbm = pl.BlockSpec(memory_space=pl.ANY)
         dma = pltpu.SemaphoreType.DMA
@@ -551,16 +478,11 @@
                 pltpu.VMEM((keys, 4, LANES), F32),
                 pltpu.VMEM((queries, HP, keys), F32),
                 pltpu.VMEM((queries, HP, keys), F32),
-                pltpu.VMEM((queries, HP, CZ), F32),
-                pltpu.VMEM((INNER, HP, LANES), F32),
-                pltpu.VMEM((sizes[1] // INNER, HP, LANES), F32),
-                pltpu.VMEM((queries, 4, LANES), F32),
-                pltpu.VMEM((sizes[1], rows, 4, LANES), F32),
-                pltpu.VMEM((queries, CS // LANES, LANES), F32),
-                pltpu.VMEM((sizes[1], rows, CS // LANES, LANES), F32),
+                pltpu.VMEM((queries, HP, LANES), F32),
+                pltpu.VMEM((sizes[1], rows, HP, LANES), F32),
                 dma((8,)),
-                dma((8,)),
-                dma((8,)),
+                dma((4,)),
+                dma((4,)),
             ],
             compiler_params=pltpu.CompilerParams(
                 collective_id=0, has_side_effects=True, vmem_limit_bytes=60 * 2**20

time: 44.7 us -> 53.9 us (1.21)
  the two profiles are of different devices: /device:TPU:56 before, /device:TPU:1 now
where the time goes in v5:
time: 53.9 us; the launch traced here: 53.7 us
  Pallas kernels  52.4 us (97%)
  local copies, waits for them, and re-layouts  1.29 us (2%)
    pallas_call x1, Pallas kernels, body(): pl.pallas_call(functools.partial(kernel, sizes), out_shape=jax.ShapeDtype...  52.4 us
    unnamed x1, local copies, waits for them, and re-layouts  1.29 us

profile of v5, /device:TPU:1, one launch (start us, length us, event | category | flops | bytes accessed | tf_op | source)
XLA Modules:
  0.0 53.7 jit_solution(2348075929440822282)
XLA Ops:
  0.0 52.4 %shard_map.82 = f32[3,384]{1,0:T(4,128)} custom-call(bf16[3,384]{1,0:T(4,128)(2,1)} %singles_hbm.1, f32[3,12]{1,0:T(4,128)} %frames_hbm.1, f32[12,128]{1,0:T(8,128)} %bitcast.6, f32[1,12]{1,0:T(1,128)} %bitcast.7, f32[96,48,128]{2,1,0:T(8,128)} %pair_hbm.1, bf16[336,384]{1,0:T(8,128)(2,1)} %bitcast.5, bf16[816,384]{1,0:T(8,128)(2,1)} %bitcast.4, ...), custom_call_target="tpu_custom_call" | custom-call | tf_op jit(solution)/shard_map/pallas_call | solution.py:458
  52.4 1.3 %copy.10 = f32[3,384]{1,0:T(4,128)} copy(f32[3,384]{1,0:T(4,128)} %shard_map.82) | data formatting | bytes 9216

commit v6 on v5

--- a/solution.py
+++ b/solution.py
@@ -92,6 +92,10 @@
     v_all,
     bias_ref,
     attn_ref,
+    pooled_ref,
+    lse_all,
+    point_own,
+    point_all,
     part_own,
     part_all,
     load_sem,
@@ -105,36 +109,36 @@
     row = lax.axis_index("row")
     col = lax.axis_index("col")
 
-    me = row * col_devs + col
-    key_col = me // owners
-    key_slot = lax.rem(me, owners)
+    core = lax.rem(row, 2)
+    partner = row + 1 - 2 * core
+    key_slot = lax.rem(col, owners)
+    source_row = col * owners // col_devs
+    first_source = lax.rem(col * owners, col_devs)
+    direct = lax.rem(source_row, 2) == core
+
+    key_col = (row * col_devs + col) // owners
     own_keys = key_col == col
-
-    def source_of(slot):
-        index = col * owners + slot
-        return (index // col_devs, lax.rem(index, col_devs))
+    other_keys = jnp.logical_not(own_keys)
 
     def far_first(count):
         return sorted(range(1, count), key=lambda step: abs(step - count // 2))
 
-    row_peers = [lax.rem(col + step, col_devs) for step in far_first(col_devs)]
+    row_peers = [(row, lax.rem(col + step, col_devs)) for step in far_first(col_devs)]
+    key_peers = [(lax.rem(row + step, row_devs), key_col) for step in far_first(row_devs)]
     barrier = pltpu.get_barrier_semaphore()
 
     def greet(peer):
         pl.semaphore_signal(barrier, inc=1, device_id=peer, device_id_type=MESH)
 
-    def greet_source(step, carry):
-        slot = lax.rem(key_slot + step, owners)
-
-        @pl.when(jnp.logical_not(jnp.logical_and(own_keys, slot == key_slot)))
-        def _():
-            greet(source_of(slot))
-
-        return carry
-
-    lax.fori_loop(0, owners, greet_source, 0)
-    for peer in row_peers:
-        greet((row, peer))
+    for step in far_first(owners):
+        greet((source_row, first_source + lax.rem(key_slot + step, owners)))
+
+    @pl.when(other_keys)
+    def _():
+        greet((source_row, first_source + key_slot))
+
+    for peer in row_peers + [(partner, col)]:
+        greet(peer)
 
     moves = [
         (singles_hbm, singles_ref),
@@ -232,7 +236,6 @@
     )
 
     own_rows = pl.ds(col * rows, rows)
-    key_rows = pl.ds(key_slot * rows, rows)
     for t in range(FEAT // LANES):
         part = slice(t * LANES, (t + 1) * LANES)
         q_all[own_rows, t, :] = q_feat[0:rows, part]
@@ -249,7 +252,7 @@
         for t in range(4):
             v_all[key_rows, t, :] = v_feat[:, t * LANES : (t + 1) * LANES]
 
-    pl.semaphore_wait(barrier, owners + col_devs - 1 - own_keys.astype(jnp.int32))
+    pl.semaphore_wait(barrier, owners + col_devs - own_keys.astype(jnp.int32))
 
     def remote(src, dst, peer, kind):
         return pltpu.make_async_remote_copy(
@@ -262,38 +265,33 @@
         )
 
     def sent(ref, kind):
-        remote(ref, ref, (row, row_peers[0]), kind).wait_send()
+        remote(ref, ref, (partner, col), kind).wait_send()
 
     def received(ref, kind):
-        remote(ref, ref, (row, row_peers[0]), kind).wait_recv()
-
-    K, Q, V, PART = range(4)
+        remote(ref, ref, (partner, col), kind).wait_recv()
+
+    K, Q, V, RELAY, LSE, POINT, PART = range(7)
     peers = col_devs - 1
-
-    def send_keys(src, dst, kind):
-        def body(step, carry):
-            peer_row = lax.rem(row + row_devs // 2 + step, row_devs)
-
-            @pl.when(jnp.logical_not(jnp.logical_and(own_keys, peer_row == row)))
-            def _():
-                remote(src, dst.at[key_rows], (peer_row, key_col), kind).start()
-
-            return carry
-
-        lax.fori_loop(0, row_devs, body, 0)
 
     def of_others(act, ref, count, kind):
         @pl.when(own_keys)
         def _():
             act(ref.at[pl.ds(0, (count - 1) * rows)], kind)
 
-        @pl.when(jnp.logical_not(own_keys))
+        @pl.when(other_keys)
         def _():
             act(ref.at[pl.ds(0, count * rows)], kind)
 
-    send_keys(k_own, k_all, K)
+    for peer in key_peers:
+        remote(k_own, k_all.at[key_rows], peer, K).start()
+
+    @pl.when(other_keys)
+    def _():
+        remote(k_own, k_all.at[key_rows], (row, key_col), K).start()
+
     for peer in row_peers:
-        remote(q_all.at[own_rows], q_all.at[own_rows], (row, peer), Q).start()
+        mine = q_all.at[own_rows]
+        remote(mine, mine, peer, Q).start()
 
     loads[5].wait()
     bias_rows = jnp.concatenate([w_bias_ref[...] * SCALE, jnp.zeros((HP - H, CZ), F32)], 0)
@@ -314,9 +312,15 @@
 
     blocks = queries // 8
     pl.loop(0, blocks // 2)(bias_block)
-    send_keys(v_own, v_all, V)
+    for step in range(2, row_devs, 2):
+        peer = (lax.rem(row + step, row_devs), key_col)
+        remote(v_own, v_all.at[key_rows], peer, V).start()
+
+    @pl.when(other_keys)
+    def _():
+        remote(v_own, v_all.at[key_rows], (row, key_col), V).start()
+
     pl.loop(blocks // 2, blocks)(bias_block)
-
     of_others(received, k_all, owners, K)
     received(q_all.at[pl.ds(0, peers * rows)], Q)
 
@@ -339,7 +343,31 @@
             attn_ref[:, h, :] = exponent * (1.0 / total)
             lse = jnp.where(lane128 == lse_lane + h, top + jnp.log(total), lse)
 
-    of_others(received, v_all, owners, V)
+    turned = jnp.concatenate([lse, jnp.zeros((LANES - queries, LANES), F32)], 0).T
+    own_lse = turned[lse_lane : lse_lane + HP]
+    lse_all[col] = own_lse
+    for peer in row_peers:
+        mine = lse_all.at[col, pl.ds(0, H)]
+        remote(mine, mine, peer, LSE).start()
+
+    @pl.when(direct)
+    def _():
+        of_others(received, v_all, owners, V)
+        remote(v_all, v_all, (partner, col), RELAY).start()
+
+    @pl.loop(0, queries // 8)
+    def _(block):
+        for u in range(8):
+            i = block * 8 + u
+            stacked = jnp.concatenate(pieces(attn_ref[i], 2), 0).astype(BF16)
+            high = dot(stacked, pair_hi[i], NN)
+            low = dot(stacked[0:HP], pair_lo[i], NN)
+            pooled_ref[i] = high[0:HP] + (high[HP:] + low)
+
+    @pl.when(jnp.logical_not(direct))
+    def _():
+        received(v_all, RELAY)
+
     values = jnp.concatenate([v_all[:, t, :] for t in range(4)], 1)
     v1, v2 = [piece.astype(BF16) for piece in pieces(values, 2)]
     lane_of = value_head(iota((1, 4 * LANES), 1))
@@ -355,46 +383,50 @@
         tile = gathered[:, t * LANES : (t + 1) * LANES]
         if t == 3:
             tile = jnp.where(lane128 >= lse_lane, lse, tile)
-        part_own[:, HP - 4 + t, :] = tile
-
-    def pool(n, carry):
-        half = col_devs // 2
-        steps = [half + 2 * n, half - 1 - 2 * n, half + 2 * n + 1, half - 2 - 2 * n]
-        to = [lax.rem(col + step, col_devs) for step in steps]
-        for owner in to:
-            for i in range(rows):
-                at = owner * rows + i
-                stacked = jnp.concatenate(pieces(attn_ref[at], 2), 0).astype(BF16)
-                high = dot(stacked, pair_hi[at], NN)
-                low = dot(stacked[0:HP], pair_lo[at], NN)
-                part_own[at, 0:H, :] = (high[0:HP] + (high[HP:] + low))[0:H]
-        for owner in to:
-
-            @pl.when(owner != col)
-            def _():
-                theirs = part_own.at[pl.ds(owner * rows, rows)]
-                remote(theirs, part_all.at[col], (row, owner), PART).start()
-
-        return carry
-
-    lax.fori_loop(0, col_devs // 4, pool, 0)
+        point_own[:, t, :] = tile
+    for i in range(rows):
+        point_all[col, i] = point_own[col * rows + i]
+    for peer in row_peers:
+        theirs = point_own.at[pl.ds(peer[1] * rows, rows)]
+        remote(theirs, point_all.at[col], peer, POINT).start()
+
+    loads[7].wait()
+    received(lse_all.at[pl.ds(0, peers), pl.ds(0, H)], LSE)
+    everyone = lse_all[...]
+    top = jnp.max(everyone, axis=0)
+    whole = top + jnp.log(jnp.sum(jnp.exp(everyone - top[None]), axis=0))
+    factor = jnp.exp(own_lse - whole)
+    factor = jnp.concatenate([factor, jnp.zeros((LANES - HP, LANES), F32)], 0).T
+    projected = jnp.zeros((queries, CS), F32)
+    for h in range(0, H, 2):
+        scaled = jnp.concatenate(
+            [pooled_ref[:, g, :] * factor[0:queries, g : g + 1] for g in (h, h + 1)], 1
+        )
+        stacked = jnp.concatenate(pieces(scaled, 2), 0).astype(BF16)
+        share = dot(stacked, w_out_ref[SPLIT + h * CZ : SPLIT + (h + 2) * CZ, :], NN)
+        projected = projected + (share[0:queries] + share[queries:])
+    for t in range(CS // LANES):
+        part_own[:, t, :] = projected[:, t * LANES : (t + 1) * LANES]
     for i in range(rows):
         part_all[col, i] = part_own[col * rows + i]
+    for peer in row_peers:
+        theirs = part_own.at[pl.ds(peer[1] * rows, rows)]
+        remote(theirs, part_all.at[col], peer, PART).start()
 
     spread = iota((LANES, 4 * LANES), 0) - lse_lane == value_head(
         iota((LANES, 4 * LANES), 1)
     )
     spread = jnp.logical_and(spread, iota((LANES, 4 * LANES), 0) >= lse_lane)
     spread = jnp.where(spread, 1.0, 0.0).astype(BF16)
-    loads[7].wait()
-    received(part_all.at[pl.ds(0, peers)], PART)
+    received(point_all.at[pl.ds(0, peers)], POINT)
     shares = []
     for i in range(rows):
-        sums = part_all[:, i, HP - 1, :]
+        sums = point_all[:, i, 3, :]
         share = jnp.exp(sums - jnp.max(sums, axis=0, keepdims=True))
         shares.append(share / jnp.sum(share, axis=0, keepdims=True))
     count = rows * col_devs
-    wide = dot(jnp.concatenate(pieces(jnp.concatenate(shares, 0), 2), 0).astype(BF16), spread, NN)
+    shares = jnp.concatenate(pieces(jnp.concatenate(shares, 0), 2), 0).astype(BF16)
+    wide = dot(shares, spread, NN)
     wide = wide[0:count] + wide[count:]
 
     def over_devices(tiles):
@@ -403,7 +435,7 @@
     kept = jnp.concatenate(
         [
             over_devices(
-                part_all[:, i, HP - 4 + t, :]
+                point_all[:, i, t, :]
                 * wide[i * col_devs : (i + 1) * col_devs, t * LANES : (t + 1) * LANES]
                 for i in range(rows)
             )
@@ -411,20 +443,6 @@
         ],
         1,
     )
-    pooled = jnp.concatenate(
-        [
-            over_devices(
-                part_all[:, i, h, :] * shares[i][:, lse_lane + h : lse_lane + h + 1]
-                for i in range(rows)
-            )
-            for h in range(H)
-        ],
-        1,
-    )
-    pooled = jnp.concatenate([pooled, jnp.zeros((8 - rows, H * CZ), F32)], 0)
-    pooled = jnp.concatenate(pieces(pooled, 2), 0).astype(BF16)
-    projected = dot(pooled, w_out_ref[SPLIT:, :], NN)
-    projected = projected[0:rows] + projected[8 : 8 + rows]
     wide = H * PV
     relative = [
         kept[:, SCALAR + b * wide : SCALAR + (b + 1) * wide] - frame[:, 9 + b : 10 + b]
@@ -438,11 +456,24 @@
     ]
     length = jnp.sqrt(local[0] ** 2 + local[1] ** 2 + local[2] ** 2 + 1.0)
     features = jnp.concatenate([kept[:, :SCALAR]] + local + [length], 1).astype(BF16)
-    out_ref[...] = dot(features, w_out_ref[0:SPLIT, :], NN) + projected
+    update = dot(features, w_out_ref[0:SPLIT, :], NN)
+
+    received(part_all.at[pl.ds(0, peers)], PART)
+    for t in range(CS // LANES):
+        part = slice(t * LANES, (t + 1) * LANES)
+        terms = over_devices(part_all[:, i, t, :] for i in range(rows))
+        out_ref[:, part] = update[:, part] + terms
 
     of_others(sent, k_all, row_devs, K)
-    of_others(sent, v_all, row_devs, V)
+    of_others(sent, v_all, row_devs // 2, V)
     sent(q_all.at[pl.ds(0, peers * rows)], Q)
+
+    @pl.when(direct)
+    def _():
+        sent(v_all, RELAY)
+
+    sent(lse_all.at[pl.ds(0, peers), pl.ds(0, H)], LSE)
+    sent(point_all.at[pl.ds(0, peers)], POINT)
     sent(part_all.at[pl.ds(0, peers)], PART)
 
 
@@ -478,11 +509,15 @@
                 pltpu.VMEM((keys, 4, LANES), F32),
                 pltpu.VMEM((queries, HP, keys), F32),
                 pltpu.VMEM((queries, HP, keys), F32),
-                pltpu.VMEM((queries, HP, LANES), F32),
-                pltpu.VMEM((sizes[1], rows, HP, LANES), F32),
+                pltpu.VMEM((queries, HP, CZ), F32),
+                pltpu.VMEM((sizes[1], HP, LANES), F32),
+                pltpu.VMEM((queries, 4, LANES), F32),
+                pltpu.VMEM((sizes[1], rows, 4, LANES), F32),
+                pltpu.VMEM((queries, CS // LANES, LANES), F32),
+                pltpu.VMEM((sizes[1], rows, CS // LANES, LANES), F32),
                 dma((8,)),
-                dma((4,)),
-                dma((4,)),
+                dma((7,)),
+                dma((7,)),
             ],
             compiler_params=pltpu.CompilerParams(
                 collective_id=0, has_side_effects=True, vmem_limit_bytes=60 * 2**20

time: 53.9 us -> 45 us (0.83)
  Pallas kernels: 52.4 us -> 43.6 us
    pallas_call x1, Pallas kernels: 52.4 us -> 43.6 us  [body(): pl.pallas_call(functools.partial(kernel, sizes), out_shape=jax.ShapeDtype...]
where the time goes in v6:
time: 45 us; the launch traced here: 44.9 us
  Pallas kernels  43.6 us (97%)
  local copies, waits for them, and re-layouts  1.29 us (3%)
    pallas_call x1, Pallas kernels, body(): pl.pallas_call(functools.partial(kernel, sizes), out_shape=jax.ShapeDtype...  43.6 us
    unnamed x1, local copies, waits for them, and re-layouts  1.29 us

profile of v6, /device:TPU:1, one launch (start us, length us, event | category | flops | bytes accessed | tf_op | source)
XLA Modules:
  0.0 44.9 jit_solution(3909664908271034844)
XLA Ops:
  0.0 43.6 %shard_map.82 = f32[3,384]{1,0:T(4,128)} custom-call(bf16[3,384]{1,0:T(4,128)(2,1)} %singles_hbm.1, f32[3,12]{1,0:T(4,128)} %frames_hbm.1, f32[12,128]{1,0:T(8,128)} %bitcast.6, f32[1,12]{1,0:T(1,128)} %bitcast.7, f32[96,48,128]{2,1,0:T(8,128)} %pair_hbm.1, bf16[336,384]{1,0:T(8,128)(2,1)} %bitcast.5, bf16[816,384]{1,0:T(8,128)(2,1)} %bitcast.4, ...), custom_call_target="tpu_custom_call" | custom-call | tf_op jit(solution)/shard_map/pallas_call | solution.py:489
  43.6 1.3 %copy.10 = f32[3,384]{1,0:T(4,128)} copy(f32[3,384]{1,0:T(4,128)} %shard_map.82) | data formatting | bytes 9216

commit v7 on v6

--- a/solution.py
+++ b/solution.py
@@ -21,6 +21,7 @@
 VALUE = SCALAR + 3 * H * PV
 SPLIT = H * (CH + 4 * PV)
 GROUP = 32
+INNER = 4
 FEAT = H * GROUP
 SCALE = math.sqrt(1.0 / 3.0)
 MESH = pl.DeviceIdType.MESH
@@ -95,7 +96,9 @@
     pooled_ref,
     lse_all,
     point_own,
-    point_all,
+    point_inner,
+    point_mid,
+    point_outer,
     part_own,
     part_all,
     load_sem,
@@ -111,6 +114,9 @@
 
     core = lax.rem(row, 2)
     partner = row + 1 - 2 * core
+    outer_devs = col_devs // INNER
+    inner = lax.rem(col, INNER)
+    outer = col // INNER
     key_slot = lax.rem(col, owners)
     source_row = col * owners // col_devs
     first_source = lax.rem(col * owners, col_devs)
@@ -124,6 +130,7 @@
         return sorted(range(1, count), key=lambda step: abs(step - count // 2))
 
     row_peers = [(row, lax.rem(col + step, col_devs)) for step in far_first(col_devs)]
+    inner_steps, outer_steps = far_first(INNER), far_first(outer_devs)
     key_peers = [(lax.rem(row + step, row_devs), key_col) for step in far_first(row_devs)]
     barrier = pltpu.get_barrier_semaphore()
 
@@ -270,7 +277,7 @@
     def received(ref, kind):
         remote(ref, ref, (partner, col), kind).wait_recv()
 
-    K, Q, V, RELAY, LSE, POINT, PART = range(7)
+    K, Q, V, RELAY, LSE, POINT_INNER, POINT_OUTER, PART = range(8)
     peers = col_devs - 1
 
     def of_others(act, ref, count, kind):
@@ -384,11 +391,19 @@
         if t == 3:
             tile = jnp.where(lane128 >= lse_lane, lse, tile)
         point_own[:, t, :] = tile
-    for i in range(rows):
-        point_all[col, i] = point_own[col * rows + i]
-    for peer in row_peers:
-        theirs = point_own.at[pl.ds(peer[1] * rows, rows)]
-        remote(theirs, point_all.at[col], peer, POINT).start()
+    for z in range(outer_devs):
+        for i in range(rows):
+            at = (z * INNER + inner) * rows + i
+            point_inner[inner, z * rows + i] = point_own[at]
+    for step in inner_steps:
+        theirs = lax.rem(inner + step, INNER)
+        for z in range(outer_devs):
+            remote(
+                point_own.at[pl.ds((z * INNER + theirs) * rows, rows)],
+                point_inner.at[inner, pl.ds(z * rows, rows)],
+                (row, outer * INNER + theirs),
+                POINT_INNER,
+            ).start()
 
     loads[7].wait()
     received(lse_all.at[pl.ds(0, peers), pl.ds(0, H)], LSE)
@@ -418,25 +433,53 @@
     )
     spread = jnp.logical_and(spread, iota((LANES, 4 * LANES), 0) >= lse_lane)
     spread = jnp.where(spread, 1.0, 0.0).astype(BF16)
-    received(point_all.at[pl.ds(0, peers)], POINT)
+
+    def spread_heads(shares):
+        wide = dot(jnp.concatenate(pieces(shares, 2), 0).astype(BF16), spread, NN)
+        return wide[0 : shares.shape[0]] + wide[shares.shape[0] :]
+
+    received(point_inner.at[pl.ds(0, INNER - 1)], POINT_INNER)
+    count = outer_devs * rows
+    sums = [point_inner[d, :, 3, :] for d in range(INNER)]
+    top = functools.reduce(jnp.maximum, sums)
+    shares = [jnp.exp(value - top) for value in sums]
+    total = sum(shares)
+    wide = spread_heads(jnp.concatenate([share / total for share in shares], 0))
+    for t in range(4):
+        tile = sum(
+            point_inner[d, :, t, :]
+            * wide[d * count : (d + 1) * count, t * LANES : (t + 1) * LANES]
+            for d in range(INNER)
+        )
+        if t == 3:
+            tile = jnp.where(lane128 >= lse_lane, top + jnp.log(total), tile)
+        point_mid[:, t, :] = tile
+    for i in range(rows):
+        point_outer[outer, i] = point_mid[outer * rows + i]
+    for step in outer_steps:
+        theirs = lax.rem(outer + step, outer_devs)
+        remote(
+            point_mid.at[pl.ds(theirs * rows, rows)],
+            point_outer.at[outer],
+            (row, theirs * INNER + inner),
+            POINT_OUTER,
+        ).start()
+
+    def over_devices(tiles):
+        return jnp.concatenate([jnp.sum(tile, axis=0, keepdims=True) for tile in tiles], 0)
+
+    received(point_outer.at[pl.ds(0, outer_devs - 1)], POINT_OUTER)
     shares = []
     for i in range(rows):
-        sums = point_all[:, i, 3, :]
+        sums = point_outer[:, i, 3, :]
         share = jnp.exp(sums - jnp.max(sums, axis=0, keepdims=True))
         shares.append(share / jnp.sum(share, axis=0, keepdims=True))
-    count = rows * col_devs
-    shares = jnp.concatenate(pieces(jnp.concatenate(shares, 0), 2), 0).astype(BF16)
-    wide = dot(shares, spread, NN)
-    wide = wide[0:count] + wide[count:]
-
-    def over_devices(tiles):
-        return jnp.concatenate([jnp.sum(tile, axis=0, keepdims=True) for tile in tiles], 0)
-
+    wide = spread_heads(jnp.concatenate(shares, 0))
     kept = jnp.concatenate(
         [
             over_devices(
-                point_all[:, i, t, :]
-                * wide[i * col_devs : (i + 1) * col_devs, t * LANES : (t + 1) * LANES]
+                point_outer[:, i, t, :]
+                * wide[i * outer_devs : (i + 1) * outer_devs, t * LANES : (t + 1) * LANES]
                 for i in range(rows)
             )
             for t in range(4)
@@ -473,7 +516,8 @@
         sent(v_all, RELAY)
 
     sent(lse_all.at[pl.ds(0, peers), pl.ds(0, H)], LSE)
-    sent(point_all.at[pl.ds(0, peers)], POINT)
+    sent(point_inner.at[pl.ds(0, INNER - 1)], POINT_INNER)
+    sent(point_outer.at[pl.ds(0, outer_devs - 1)], POINT_OUTER)
     sent(part_all.at[pl.ds(0, peers)], PART)
 
 
@@ -512,12 +556,14 @@
                 pltpu.VMEM((queries, HP, CZ), F32),
                 pltpu.VMEM((sizes[1], HP, LANES), F32),
                 pltpu.VMEM((queries, 4, LANES), F32),
-                pltpu.VMEM((sizes[1], rows, 4, LANES), F32),
+                pltpu.VMEM((INNER, sizes[1] // INNER * rows, 4, LANES), F32),
+                pltpu.VMEM((sizes[1] // INNER * rows, 4, LANES), F32),
+                pltpu.VMEM((sizes[1] // INNER, rows, 4, LANES), F32),
                 pltpu.VMEM((queries, CS // LANES, LANES), F32),
                 pltpu.VMEM((sizes[1], rows, CS // LANES, LANES), F32),
                 dma((8,)),
-                dma((7,)),
-                dma((7,)),
+                dma((8,)),
+                dma((8,)),
             ],
             compiler_params=pltpu.CompilerParams(
                 collective_id=0, has_side_effects=True, vmem_limit_bytes=60 * 2**20

time: 45 us -> 43.8 us (0.973); the launches traced: 44.9 us -> 43 us
  Pallas kernels: 43.6 us -> 41.7 us
    pallas_call x1, Pallas kernels: 43.6 us -> 41.7 us  [body(): pl.pallas_call(functools.partial(kernel, sizes), out_shape=jax.ShapeDtype...]
where the time goes in v7:
time: 43.8 us; the launch traced here: 43 us
  Pallas kernels  41.7 us (95%)
  local copies, waits for them, and re-layouts  1.29 us (3%)
    pallas_call x1, Pallas kernels, body(): pl.pallas_call(functools.partial(kernel, sizes), out_shape=jax.ShapeDtype...  41.7 us
    unnamed x1, local copies, waits for them, and re-layouts  1.29 us

profile of v7, /device:TPU:1, one launch (start us, length us, event | category | flops | bytes accessed | tf_op | source)
XLA Modules:
  0.0 43.0 jit_solution(9480635537621186656)
XLA Ops:
  0.0 41.7 %shard_map.82 = f32[3,384]{1,0:T(4,128)} custom-call(bf16[3,384]{1,0:T(4,128)(2,1)} %singles_hbm.1, f32[3,12]{1,0:T(4,128)} %frames_hbm.1, f32[12,128]{1,0:T(8,128)} %bitcast.6, f32[1,12]{1,0:T(1,128)} %bitcast.7, f32[96,48,128]{2,1,0:T(8,128)} %pair_hbm.1, bf16[336,384]{1,0:T(8,128)(2,1)} %bitcast.5, bf16[816,384]{1,0:T(8,128)(2,1)} %bitcast.4, ...), custom_call_target="tpu_custom_call" | custom-call | tf_op jit(solution)/shard_map/pallas_call | solution.py:533
  41.7 1.3 %copy.10 = f32[3,384]{1,0:T(4,128)} copy(f32[3,384]{1,0:T(4,128)} %shard_map.82) | data formatting | bytes 9216

commit v8 on v7

--- a/solution.py
+++ b/solution.py
@@ -362,10 +362,10 @@
         of_others(received, v_all, owners, V)
         remote(v_all, v_all, (partner, col), RELAY).start()
 
-    @pl.loop(0, queries // 8)
+    @pl.loop(0, queries // 24)
     def _(block):
-        for u in range(8):
-            i = block * 8 + u
+        for u in range(24):
+            i = block * 24 + u
             stacked = jnp.concatenate(pieces(attn_ref[i], 2), 0).astype(BF16)
             high = dot(stacked, pair_hi[i], NN)
             low = dot(stacked[0:HP], pair_lo[i], NN)
@@ -378,19 +378,22 @@
     values = jnp.concatenate([v_all[:, t, :] for t in range(4)], 1)
     v1, v2 = [piece.astype(BF16) for piece in pieces(values, 2)]
     lane_of = value_head(iota((1, 4 * LANES), 1))
-    gathered = jnp.zeros((queries, 4 * LANES), F32)
-    for h in range(H):
-        mask = jnp.where(lane_of == h, 1.0, 0.0).astype(BF16)
-        a1, a2 = [piece.astype(BF16) for piece in pieces(attn_ref[:, h, :], 2)]
-        left = jnp.concatenate([a1, a2], 0)
-        high = dot(left, v1 * mask, NN)
-        low = dot(a1, v2 * mask, NN)
-        gathered = gathered + (high[0:queries] + (high[queries:] + low))
-    for t in range(4):
-        tile = gathered[:, t * LANES : (t + 1) * LANES]
-        if t == 3:
-            tile = jnp.where(lane128 >= lse_lane, lse, tile)
-        point_own[:, t, :] = tile
+    for t in range(0, 4, 2):
+        part = slice(t * LANES, (t + 2) * LANES)
+        gathered = jnp.zeros((queries, 2 * LANES), F32)
+        for h in range(H):
+            mask = jnp.where(lane_of[:, part] == h, 1.0, 0.0).astype(BF16)
+            a1, a2 = [piece.astype(BF16) for piece in pieces(attn_ref[:, h, :], 2)]
+            high = dot(jnp.concatenate([a1, a2], 0), v1[:, part] * mask, NN)
+            low = dot(a1, v2[:, part] * mask, NN)
+            gathered = gathered + (high[0:queries] + (high[queries:] + low))
+        if t == 0:
+            point_own[:, 0, :] = gathered[:, 0:LANES]
+            point_own[:, 1, :] = gathered[:, LANES:]
+        else:
+            last = gathered[:, LANES:]
+            point_own[:, 2, :] = gathered[:, 0:LANES]
+            point_own[:, 3, :] = jnp.where(lane128 >= lse_lane, lse, last)
     for z in range(outer_devs):
         for i in range(rows):
             at = (z * INNER + inner) * rows + i
@@ -532,7 +535,7 @@
         dma = pltpu.SemaphoreType.DMA
         return pl.pallas_call(
             functools.partial(kernel, sizes),
-            out_shape=jax.ShapeDtypeStruct((rows, w_out.shape[1]), F32),
+            out_shape=pltpu.VMEM((rows, w_out.shape[1]), F32),
             in_specs=[hbm] * 8,
             out_specs=vmem,
             scratch_shapes=[

time: 43.8 us -> 42.5 us (0.970)
  local copies, waits for them, and re-layouts: 1.29 us -> 0.6 us
  Pallas kernels: 41.7 us -> 41.2 us
    unnamed x1, local copies, waits for them, and re-layouts: 1.29 us -> 0.6 us
    pallas_call x1, Pallas kernels: 41.7 us -> 41.2 us  [body(): pl.pallas_call(functools.partial(kernel, sizes), out_shape=pltpu.VMEM((ro...]
where the time goes in v8:
time: 42.5 us; the launch traced here: 41.8 us
  Pallas kernels  41.2 us (97%)
  local copies, waits for them, and re-layouts  0.6 us (1%)
    pallas_call x1, Pallas kernels, body(): pl.pallas_call(functools.partial(kernel, sizes), out_shape=pltpu.VMEM((ro...  41.2 us

profile of v8, /device:TPU:1, one launch (start us, length us, event | category | flops | bytes accessed | tf_op | source)
XLA Modules:
  0.0 41.8 jit_solution(4273051818289263169)
XLA Ops:
  0.0 41.2 %shard_map.82 = f32[3,384]{1,0:T(4,128)S(1)} custom-call(bf16[3,384]{1,0:T(4,128)(2,1)} %singles_hbm.1, f32[3,12]{1,0:T(4,128)} %frames_hbm.1, f32[12,128]{1,0:T(8,128)} %bitcast.6, f32[1,12]{1,0:T(1,128)} %bitcast.7, f32[96,48,128]{2,1,0:T(8,128)} %pair_hbm.1, bf16[336,384]{1,0:T(8,128)(2,1)} %bitcast.5, bf16[816,384]{1,0:T(8,128)(2,1)} %bitcast.4, ...), custom_call_target="tpu_custom_call" | custom-call | tf_op jit(solution)/shard_map/pallas_call | solution.py:536
  41.2 0.6 %copy.10 = f32[3,384]{1,0:T(4,128)} copy(f32[3,384]{1,0:T(4,128)S(1)} %shard_map.82) | data formatting | bytes 9216

commit v9 on v8

--- a/solution.py
+++ b/solution.py
@@ -16,6 +16,7 @@
 PV = 8
 
 HP = 16
+PITCH = 24
 LANES = 128
 SCALAR = H * CH
 VALUE = SCALAR + 3 * H * PV
@@ -315,7 +316,7 @@
             second = dot(bias_pieces[0 : 2 * HP], middle, NT)
             third = dot(bias_pieces[0:HP], low, NT)
             small = first[2 * HP :] + second[HP:] + third
-            bias_ref[i] = first[0:HP] + (first[HP : 2 * HP] + second[0:HP] + small)
+            bias_ref[i, 0:HP, :] = first[0:HP] + (first[HP : 2 * HP] + second[0:HP] + small)
 
     blocks = queries // 8
     pl.loop(0, blocks // 2)(bias_block)
@@ -334,16 +335,25 @@
     lse_lane = VALUE % LANES
     lane128 = iota((1, LANES), 1)
     lse = jnp.zeros((queries, LANES), F32)
+    per_tile = LANES // GROUP
+    tile_head = lax.rem(iota((6 * LANES, keys), 0), LANES) // GROUP
+
+    def inner_products(t):
+        q1, q2, q3 = [piece.astype(BF16) for piece in pieces(q_all[:, t, :], 3)]
+        k1, k2, k3 = [piece.astype(BF16) for piece in pieces(k_all[:, t, :].T, 3)]
+        left = jnp.concatenate([q1, q1, q2, q1, q2, q3], 1)
+        right = jnp.concatenate([k1, k2, k1, k3, k2, k1], 0)
+        masks = [jnp.where(tile_head == g, 1.0, 0.0).astype(BF16) for g in range(per_tile)]
+        return [dot(left, right * mask, NN) for mask in masks]
+
+    coming = inner_products(0)
     for t in range(FEAT // LANES):
-        q1, q2, q3 = [piece.astype(BF16) for piece in pieces(q_all[:, t, :], 3)]
-        k1, k2, k3 = [piece.astype(BF16) for piece in pieces(k_all[:, t, :], 3)]
-        left = jnp.concatenate([q1, q1, q2, q1, q2, q3], 1)
-        right = jnp.concatenate([k1, k2, k1, k3, k2, k1], 1)
-        tile_head = lax.rem(iota((1, 6 * LANES), 1), LANES) // GROUP
-        for g in range(LANES // GROUP):
-            h = t * (LANES // GROUP) + g
-            mask = jnp.where(tile_head == g, 1.0, 0.0).astype(BF16)
-            logits = dot(left, right * mask, NT) + bias_ref[:, h, :]
+        products = coming
+        if (t + 1) * LANES < FEAT:
+            coming = inner_products(t + 1)
+        for g in range(per_tile):
+            h = t * per_tile + g
+            logits = products[g] + bias_ref[:, h, :]
             top = jnp.max(logits, axis=1, keepdims=True)
             exponent = jnp.exp(logits - top)
             total = jnp.sum(exponent, axis=1, keepdims=True)
@@ -366,10 +376,10 @@
     def _(block):
         for u in range(24):
             i = block * 24 + u
-            stacked = jnp.concatenate(pieces(attn_ref[i], 2), 0).astype(BF16)
+            stacked = jnp.concatenate(pieces(attn_ref[i, 0:HP, :], 2), 0).astype(BF16)
             high = dot(stacked, pair_hi[i], NN)
             low = dot(stacked[0:HP], pair_lo[i], NN)
-            pooled_ref[i] = high[0:HP] + (high[HP:] + low)
+            pooled_ref[i, 0:HP, :] = high[0:HP] + (high[HP:] + low)
 
     @pl.when(jnp.logical_not(direct))
     def _():
@@ -554,9 +564,9 @@
                 pltpu.VMEM((rows, 4, LANES), F32),
                 pltpu.VMEM((keys, FEAT // LANES, LANES), F32),
                 pltpu.VMEM((keys, 4, LANES), F32),
-                pltpu.VMEM((queries, HP, keys), F32),
-                pltpu.VMEM((queries, HP, keys), F32),
-                pltpu.VMEM((queries, HP, CZ), F32),
+                pltpu.VMEM((queries, PITCH, keys), F32),
+                pltpu.VMEM((queries, PITCH, keys), F32),
+                pltpu.VMEM((queries, PITCH, CZ), F32),
                 pltpu.VMEM((sizes[1], HP, LANES), F32),
                 pltpu.VMEM((queries, 4, LANES), F32),
                 pltpu.VMEM((INNER, sizes[1] // INNER * rows, 4, LANES), F32),

time: 42.5 us -> 42.5 us (level)
  the two profiles are of different devices: /device:TPU:1 before, /device:TPU:56 now
where the time goes in v9:
time: 42.5 us; the launch traced here: 42.3 us
  Pallas kernels  41.7 us (98%)
  local copies, waits for them, and re-layouts  0.6 us (1%)
    pallas_call x1, Pallas kernels, body(): pl.pallas_call(functools.partial(kernel, sizes), out_shape=pltpu.VMEM((ro...  41.7 us

profile of v9, /device:TPU:56, one launch (start us, length us, event | category | flops | bytes accessed | tf_op | source)
XLA Modules:
  0.0 42.3 jit_solution(2547914398318208426)
XLA Ops:
  0.0 41.7 %shard_map.82 = f32[3,384]{1,0:T(4,128)S(1)} custom-call(bf16[3,384]{1,0:T(4,128)(2,1)} %singles_hbm.1, f32[3,12]{1,0:T(4,128)} %frames_hbm.1, f32[12,128]{1,0:T(8,128)} %bitcast.6, f32[1,12]{1,0:T(1,128)} %bitcast.7, f32[96,48,128]{2,1,0:T(8,128)} %pair_hbm.1, bf16[336,384]{1,0:T(8,128)(2,1)} %bitcast.5, bf16[816,384]{1,0:T(8,128)(2,1)} %bitcast.4, ...), custom_call_target="tpu_custom_call" | custom-call | tf_op jit(solution)/shard_map/pallas_call | solution.py:546
  41.7 0.6 %copy.10 = f32[3,384]{1,0:T(4,128)} copy(f32[3,384]{1,0:T(4,128)S(1)} %shard_map.82) | data formatting | bytes 9216
